TPU v7x, 32 devices: a whole 2x2x4 slice. The times are simulated.
32 devices in a mesh: tp: 4 (over z), dp: 8 (over y, x, core).
Axes of the slice: x: 2, y: 2, z: 4, core: 2. Of those that a mesh axis runs over, the one named last changes fastest.
Arguments:
- tokens: int32 [8, 1024], P('dp')
- labels: int32 [8, 1024], P('dp')
- embedding: float32 [50304, 768], P('tp')
- vec_params: float32 [16, 768], replicated
- w_qkv: float32 [2, 768, 2304], P(None, None, 'tp')
- b_qkv: float32 [2, 12, 192], P(None, 'tp')
- w_out: float32 [2, 768, 768], P(None, 'tp')
- w_up: float32 [2, 768, 3072], P(None, None, 'tp')
- b_up: float32 [2, 3072], P(None, 'tp')
- w_down: float32 [2, 3072, 768], P(None, 'tp')
- mom_embedding: float32 [50304, 768], P('tp')
- mom_vec_params: float32 [16, 768], replicated
- mom_w_qkv: float32 [2, 768, 2304], P(None, None, 'tp')
- mom_b_qkv: float32 [2, 12, 192], P(None, 'tp')
- mom_w_out: float32 [2, 768, 768], P(None, 'tp')
- mom_w_up: float32 [2, 768, 3072], P(None, None, 'tp')
- mom_b_up: float32 [2, 3072], P(None, 'tp')
- mom_w_down: float32 [2, 3072, 768], P(None, 'tp')
- vel_embedding: float32 [50304, 768], P('tp')
- vel_vec_params: float32 [16, 768], replicated
- vel_w_qkv: float32 [2, 768, 2304], P(None, None, 'tp')
- vel_b_qkv: float32 [2, 12, 192], P(None, 'tp')
- vel_w_out: float32 [2, 768, 768], P(None, 'tp')
- vel_w_up: float32 [2, 768, 3072], P(None, None, 'tp')
- vel_b_up: float32 [2, 3072], P(None, 'tp')
- vel_w_down: float32 [2, 3072, 768], P(None, 'tp')
Outputs:
- output 1: float32 [], replicated
- output 2: float32 [50304, 768], P('tp')
- output 3: float32 [16, 768], replicated
- output 4: float32 [2, 768, 2304], P(None, None, 'tp')
- output 5: float32 [2, 12, 192], P(None, 'tp')
- output 6: float32 [2, 768, 768], P(None, 'tp')
- output 7: float32 [2, 768, 3072], P(None, None, 'tp')
- output 8: float32 [2, 3072], P(None, 'tp')
- output 9: float32 [2, 3072, 768], P(None, 'tp')
- output 10: float32 [50304, 768], P('tp')
- output 11: float32 [16, 768], replicated
- output 12: float32 [2, 768, 2304], P(None, None, 'tp')
- output 13: float32 [2, 12, 192], P(None, 'tp')
- output 14: float32 [2, 768, 768], P(None, 'tp')
- output 15: float32 [2, 768, 3072], P(None, None, 'tp')
- output 16: float32 [2, 3072], P(None, 'tp')
- output 17: float32 [2, 3072, 768], P(None, 'tp')
- output 18: float32 [50304, 768], P('tp')
- output 19: float32 [16, 768], replicated
- output 20: float32 [2, 768, 2304], P(None, None, 'tp')
- output 21: float32 [2, 12, 192], P(None, 'tp')
- output 22: float32 [2, 768, 768], P(None, 'tp')
- output 23: float32 [2, 768, 3072], P(None, None, 'tp')
- output 24: float32 [2, 3072], P(None, 'tp')
- output 25: float32 [2, 3072, 768], P(None, 'tp')
- output 26: bfloat16 [50304, 768], P('tp')
- output 27: bfloat16 [16, 768], replicated
- output 28: bfloat16 [2, 768, 2304], P(None, None, 'tp')
- output 29: bfloat16 [2, 12, 192], P(None, 'tp')
- output 30: bfloat16 [2, 768, 768], P(None, 'tp')
- output 31: bfloat16 [2, 768, 3072], P(None, None, 'tp')
- output 32: bfloat16 [2, 3072], P(None, 'tp')
- output 33: bfloat16 [2, 3072, 768], P(None, 'tp')
All inputs are finite; a program needn't handle non-finite values.
Results may differ from a plain program's by a relative error of at most 0.001.
Values sent between devices are 32-bit elements.
A program may use at most 1.5 GiB of HBM per device.

v0:
```python
import math
import jax
import jax.numpy as jnp
from jax import lax
from jax.sharding import PartitionSpec as P

LN_EPS = 1e-5
CLIP_NORM = 1.0
BETA_ONE = 0.9
BETA_TWO = 0.95
ADAM_EPS = 1e-8
WEIGHT_DECAY = 0.1
LEARN_RATE = 1e-3
STEP_COUNT = 10
DECAYED = (True, False, True, False, True, True, False, True)
PARAM_SPECS = (P('tp', None), P(None, None), P(None, None, 'tp'), P(None, 'tp', None), P(None, 'tp', None), P(None, None, 'tp'), P(None, 'tp'), P(None, 'tp', None))
CONTRACT_ROWS = (((0,), (0,)), ((), ()))
CONTRACT_COLS = (((1,), (1,)), ((), ()))


def alibi_slopes(heads):
    closest = 2 ** int(math.floor(math.log2(heads)))
    first_base = 2.0 ** (-8.0 / closest)
    slopes = [first_base ** (head_idx + 1) for head_idx in range(closest)]
    extra_base = 2.0 ** (-4.0 / closest)
    extra_count = min(closest, heads - closest)
    return slopes + [extra_base ** (2 * head_idx + 1) for head_idx in range(extra_count)]


def layer_norm(values, gain, bias):
    centred = values - jnp.mean(values, axis=-1, keepdims=True)
    variance = jnp.mean(centred * centred, axis=-1, keepdims=True)
    return centred * lax.rsqrt(variance + LN_EPS) * gain + bias


def gelu_tanh(values):
    return jax.nn.gelu(values, approximate=True)


def attn_probs(query, key_blk, slopes, scale):
    seq_len = query.shape[1]
    positions = jnp.arange(seq_len)
    rel_pos = (positions[None, :] - positions[:, None]).astype(jnp.float32)
    causal = positions[None, :] <= positions[:, None]
    scores = jnp.einsum('bqhd,bkhd->bhqk', query, key_blk, preferred_element_type=jnp.float32) * scale
    scores = scores + slopes[None, :, None, None] * rel_pos[None, None]
    scores = jnp.where(causal[None, None], scores, -jnp.inf)
    return jax.nn.softmax(scores, axis=-1)


def adam_update(master, grad_arr, moment, velocity, decayed):
    mom_new = BETA_ONE * moment + (1.0 - BETA_ONE) * grad_arr
    vel_new = BETA_TWO * velocity + (1.0 - BETA_TWO) * grad_arr * grad_arr
    mom_hat = mom_new / (1.0 - BETA_ONE ** STEP_COUNT)
    vel_hat = vel_new / (1.0 - BETA_TWO ** STEP_COUNT)
    direction = mom_hat / (jnp.sqrt(vel_hat) + ADAM_EPS)
    if decayed:
        direction = direction + WEIGHT_DECAY * master
    return master - LEARN_RATE * direction, mom_new, vel_new


def local_grads(tokens, labels, masters, tp_size, dp_size):
    embedding, vec_params, w_qkv, b_qkv, w_out, w_up, b_up, w_down = masters
    tp_rank = lax.axis_index('tp')
    vocab_loc = embedding.shape[0]
    batch_loc, seq_len = tokens.shape
    n_tok = batch_loc * seq_len
    n_total = n_tok * dp_size
    layers = w_qkv.shape[0]
    heads_loc = b_qkv.shape[1]
    head_dim = b_qkv.shape[2] // 3
    scale = head_dim ** -0.5
    slope_all = jnp.array(alibi_slopes(heads_loc * tp_size), dtype=jnp.float32)
    slope_loc = lax.dynamic_slice_in_dim(slope_all, tp_rank * heads_loc, heads_loc)
    emb_b = embedding.astype(jnp.bfloat16)
    wqkv_b = w_qkv.astype(jnp.bfloat16)
    wout_b = w_out.astype(jnp.bfloat16)
    wup_b = w_up.astype(jnp.bfloat16)
    wdown_b = w_down.astype(jnp.bfloat16)

    id_local = tokens.reshape(-1) - tp_rank * vocab_loc
    in_shard = (id_local >= 0) & (id_local < vocab_loc)
    safe_ids = jnp.clip(id_local, 0, vocab_loc - 1)
    picked = jnp.take(emb_b, safe_ids, axis=0)
    x_embed = lax.psum(jnp.where(in_shard[:, None], picked.astype(jnp.float32), 0.0), 'tp')
    resid, ln_zero_vjp = jax.vjp(layer_norm, x_embed, vec_params[0], vec_params[1])

    saved = []
    for layer in range(layers):
        row_base = 2 + 6 * layer
        normed_one, ln_one_vjp = jax.vjp(layer_norm, resid, vec_params[row_base], vec_params[row_base + 1])
        act_in = normed_one.astype(jnp.bfloat16)
        qkv = (jnp.dot(act_in, wqkv_b[layer], preferred_element_type=jnp.float32) + b_qkv[layer].reshape(-1)).astype(jnp.bfloat16)
        qkv = qkv.reshape(batch_loc, seq_len, heads_loc, 3, head_dim)
        query = qkv[:, :, :, 0]
        key_blk = qkv[:, :, :, 1]
        value_blk = qkv[:, :, :, 2]
        probs = attn_probs(query, key_blk, slope_loc, scale)
        context = jnp.einsum('bhqk,bkhd->bqhd', probs.astype(jnp.bfloat16), value_blk, preferred_element_type=jnp.float32).astype(jnp.bfloat16).reshape(n_tok, heads_loc * head_dim)
        attn_out = lax.psum(jnp.dot(context, wout_b[layer], preferred_element_type=jnp.float32), 'tp') + vec_params[row_base + 2]
        mid = resid + attn_out
        normed_two, ln_two_vjp = jax.vjp(layer_norm, mid, vec_params[row_base + 3], vec_params[row_base + 4])
        mlp_in = normed_two.astype(jnp.bfloat16)
        pre_act = jnp.dot(mlp_in, wup_b[layer], preferred_element_type=jnp.float32) + b_up[layer]
        act_out, gelu_vjp = jax.vjp(gelu_tanh, pre_act)
        hidden = act_out.astype(jnp.bfloat16)
        resid = mid + lax.psum(jnp.dot(hidden, wdown_b[layer], preferred_element_type=jnp.float32), 'tp') + vec_params[row_base + 5]
        saved.append((ln_one_vjp, act_in, query, key_blk, value_blk, context, ln_two_vjp, mlp_in, gelu_vjp, hidden))

    final_row = 2 + 6 * layers
    normed_fin, ln_fin_vjp = jax.vjp(layer_norm, resid, vec_params[final_row], vec_params[final_row + 1])
    head_in = normed_fin.astype(jnp.bfloat16)
    logits = lax.dot_general(head_in, emb_b, CONTRACT_COLS, preferred_element_type=jnp.float32)
    glob_max = lax.pmax(jnp.max(logits, axis=1), 'tp')
    shifted = jnp.exp(logits - glob_max[:, None])
    sum_exp = lax.psum(jnp.sum(shifted, axis=1), 'tp')
    lab_local = labels.reshape(-1) - tp_rank * vocab_loc
    onehot = jnp.arange(vocab_loc)[None, :] == lab_local[:, None]
    target = lax.psum(jnp.sum(jnp.where(onehot, logits, 0.0), axis=1), 'tp')
    loss_sum = jnp.sum(glob_max + jnp.log(sum_exp) - target)

    d_logits = ((shifted / sum_exp[:, None] - onehot.astype(jnp.float32)) / n_total).astype(jnp.bfloat16)
    g_emb = lax.dot_general(d_logits, head_in, CONTRACT_ROWS, preferred_element_type=jnp.float32)
    d_head = lax.psum(jnp.dot(d_logits, emb_b, preferred_element_type=jnp.float32), 'tp')
    vec_grads = {}
    d_resid, vec_grads[final_row], vec_grads[final_row + 1] = ln_fin_vjp(d_head)
    g_qkv_all = {}
    g_bqkv_all = {}
    g_out_all = {}
    g_up_all = {}
    g_bup_all = {}
    g_down_all = {}
    for layer in reversed(range(layers)):
        ln_one_vjp, act_in, query, key_blk, value_blk, context, ln_two_vjp, mlp_in, gelu_vjp, hidden = saved[layer]
        row_base = 2 + 6 * layer
        vec_grads[row_base + 5] = jnp.sum(d_resid, axis=0)
        d_out = d_resid.astype(jnp.bfloat16)
        g_down_all[layer] = lax.dot_general(hidden, d_out, CONTRACT_ROWS, preferred_element_type=jnp.float32)
        d_hidden = lax.dot_general(d_out, wdown_b[layer], CONTRACT_COLS, preferred_element_type=jnp.float32)
        d_pre = gelu_vjp(d_hidden)[0]
        g_bup_all[layer] = jnp.sum(d_pre, axis=0)
        d_pre_b = d_pre.astype(jnp.bfloat16)
        g_up_all[layer] = lax.dot_general(mlp_in, d_pre_b, CONTRACT_ROWS, preferred_element_type=jnp.float32)
        d_norm_two = lax.psum(lax.dot_general(d_pre_b, wup_b[layer], CONTRACT_COLS, preferred_element_type=jnp.float32), 'tp')
        d_mid_ln, vec_grads[row_base + 3], vec_grads[row_base + 4] = ln_two_vjp(d_norm_two)
        d_mid = d_resid + d_mid_ln
        vec_grads[row_base + 2] = jnp.sum(d_mid, axis=0)
        d_attn = d_mid.astype(jnp.bfloat16)
        g_out_all[layer] = lax.dot_general(context, d_attn, CONTRACT_ROWS, preferred_element_type=jnp.float32)
        d_context = lax.dot_general(d_attn, wout_b[layer], CONTRACT_COLS, preferred_element_type=jnp.float32).astype(jnp.bfloat16).reshape(batch_loc, seq_len, heads_loc, head_dim)
        probs = attn_probs(query, key_blk, slope_loc, scale)
        d_probs = jnp.einsum('bqhd,bkhd->bhqk', d_context, value_blk, preferred_element_type=jnp.float32)
        d_value = jnp.einsum('bhqk,bqhd->bkhd', probs.astype(jnp.bfloat16), d_context, preferred_element_type=jnp.float32)
        d_scores = (probs * (d_probs - jnp.sum(probs * d_probs, axis=-1, keepdims=True)) * scale).astype(jnp.bfloat16)
        d_query = jnp.einsum('bhqk,bkhd->bqhd', d_scores, key_blk, preferred_element_type=jnp.float32)
        d_key = jnp.einsum('bhqk,bqhd->bkhd', d_scores, query, preferred_element_type=jnp.float32)
        d_qkv = jnp.stack([d_query, d_key, d_value], axis=3).reshape(n_tok, heads_loc * 3 * head_dim)
        g_bqkv_all[layer] = jnp.sum(d_qkv, axis=0).reshape(heads_loc, 3 * head_dim)
        d_qkv_b = d_qkv.astype(jnp.bfloat16)
        g_qkv_all[layer] = lax.dot_general(act_in, d_qkv_b, CONTRACT_ROWS, preferred_element_type=jnp.float32)
        d_norm_one = lax.psum(lax.dot_general(d_qkv_b, wqkv_b[layer], CONTRACT_COLS, preferred_element_type=jnp.float32), 'tp')
        d_res_ln, vec_grads[row_base], vec_grads[row_base + 1] = ln_one_vjp(d_norm_one)
        d_resid = d_mid + d_res_ln
    d_embed, vec_grads[0], vec_grads[1] = ln_zero_vjp(d_resid)
    d_rows = jnp.where(in_shard[:, None], d_embed, 0.0)
    g_emb = g_emb + jax.ops.segment_sum(d_rows, safe_ids, num_segments=vocab_loc)
    grads = [g_emb,
             jnp.stack([vec_grads[row] for row in range(final_row + 2)]),
             jnp.stack([g_qkv_all[layer] for layer in range(layers)]),
             jnp.stack([g_bqkv_all[layer] for layer in range(layers)]),
             jnp.stack([g_out_all[layer] for layer in range(layers)]),
             jnp.stack([g_up_all[layer] for layer in range(layers)]),
             jnp.stack([g_bup_all[layer] for layer in range(layers)]),
             jnp.stack([g_down_all[layer] for layer in range(layers)])]
    return loss_sum, grads


def solution(mesh):
    tp_size = mesh.shape['tp']
    dp_size = mesh.shape['dp']

    def device_step(tokens, labels, *state):
        masters = state[0:8]
        moms = state[8:16]
        vels = state[16:24]
        loss_sum, grads = local_grads(tokens, labels, masters, tp_size, dp_size)
        n_total = tokens.shape[0] * tokens.shape[1] * dp_size
        loss = lax.psum(loss_sum, 'dp') / n_total
        grads = [lax.psum(grad_arr, 'dp') for grad_arr in grads]
        sq_sharded = sum(jnp.sum(grads[slot] * grads[slot]) for slot in range(8) if slot != 1)
        sq_total = lax.psum(sq_sharded, 'tp') + jnp.sum(grads[1] * grads[1])
        clip_coef = jnp.minimum(1.0, CLIP_NORM / (jnp.sqrt(sq_total) + 1e-6))
        updated = [adam_update(masters[slot], grads[slot] * clip_coef, moms[slot], vels[slot], DECAYED[slot]) for slot in range(8)]
        new_masters = [entry[0] for entry in updated]
        new_moms = [entry[1] for entry in updated]
        new_vels = [entry[2] for entry in updated]
        new_bf16 = [entry.astype(jnp.bfloat16) for entry in new_masters]
        return (loss, *new_masters, *new_moms, *new_vels, *new_bf16)

    data_spec = P('dp', None)
    return jax.shard_map(device_step, mesh=mesh, in_specs=(data_spec, data_spec) + PARAM_SPECS * 3, out_specs=(P(),) + PARAM_SPECS * 4, check_vma=False)
```

profile of v0, /device:TPU:0, one launch (start us, length us, event | category | flops | bytes accessed | tf_op | source)
XLA Modules:
  0.0 2463.5 jit_solution(4526563361275554073)
XLA Ops:
  8.7 20.6 convert_element_type.183
  29.4 14.5 gather_fusion
  43.9 3.4 convert_select_fusion
  54.2 2.6 subtract_convert_fusion
  56.8 113.2 %all-reduce.15.cloned.1.call-done = f32[1024,768]{1,0:T(8,128)} async-done(((f32[1024,768]{1,0:T(8,128)}), f32[1024,768]{1,0:T(8,128)}) %all-reduce.15.cloned.1.call-update) | async-done | bytes 3145744 | tf_op jit(solution)/shard_map/psum | solution.py:85
  180.5 10.7 fusion.187
  191.3 6.0 fusion.99
  200.4 11.5 all-reduce.19.cloned.1.call-start
  211.9 4.0 convert_element_type.197
  215.8 4.0 convert_element_type.195
  219.9 99.6 %all-reduce.17.cloned.1.call-done = f32[1024,768]{1,0:T(8,128)} async-done(((f32[1024,768]{1,0:T(8,128)}), f32[1024,768]{1,0:T(8,128)}) %all-reduce.17.cloned.1.call-update) | async-done | bytes 3145744 | tf_op jit(solution)/shard_map/psum | solution.py:100
  319.5 2.9 fusion.186
  328.6 3.8 fusion.109
  332.5 119.0 %all-reduce.19.cloned.1.call-done = f32[1024,768]{1,0:T(8,128)} async-done(((f32[1024,768]{1,0:T(8,128)}), f32[1024,768]{1,0:T(8,128)}) %all-reduce.19.cloned.1.call-update) | async-done | bytes 3145744 | tf_op jit(solution)/shard_map/psum | solution.py:107
  451.5 3.3 fusion.185
  459.5 10.7 fusion.188
  470.3 6.0 fusion.102
  479.4 119.1 %all-reduce.21.cloned.1.call-done = f32[1024,768]{1,0:T(8,128)} async-done(((f32[1024,768]{1,0:T(8,128)}), f32[1024,768]{1,0:T(8,128)}) %all-reduce.21.cloned.1.call-update) | async-done | bytes 3145744 | tf_op jit(solution)/shard_map/psum | solution.py:100
  607.0 3.8 fusion.113
  611.0 118.8 %all-reduce.23.cloned.1.call-done = f32[1024,768]{1,0:T(8,128)} async-done(((f32[1024,768]{1,0:T(8,128)}), f32[1024,768]{1,0:T(8,128)}) %all-reduce.23.cloned.1.call-update) | async-done | bytes 3145744 | tf_op jit(solution)/shard_map/psum | solution.py:107
  734.4 31.9 %fusion.189 = (f32[1024]{0:T(1024)S(1)}, f32[1024,12576]{0,1:T(8,128)}) fusion(bf16[12576,768]{1,0:T(8,128)(2,1)} %convert_element_type.183, f32[1024,768]{1,0:T(8,128)} %copy-done.8, f32[768]{0:T(1024)S(1)} %get-tuple-element.134, f32[768]{0:T(1024)S(1)} %get-tuple-element.119, f32[1024]{0:T(1024)S(1)} %fusion.141, f32[1024]{0:T(1024)S(1)} %broadcast_multiply_fusion), kind=kOutput, calls=%fused_computation.330 | convolution fusion | flops 19797147648 | bytes 73992192 | tf_op jit(solution)/shard_map/dot_general | solution.py:113
  766.3 10.1 pmax.7
  776.4 22.3 fusion.4
  798.8 9.3 all-reduce.2
  808.1 26.5 %multiply_convert_fusion = bf16[1024,12576]{0,1:T(8,128)(2,1)} fusion(f32[1024,12576]{0,1:T(8,128)} %get-tuple-element.217, f32[1024]{0:T(1024)S(1)} %get-tuple-element.149, s32[1024]{0:T(1024)S(1)} %bitcast.236, f32[1024]{0:T(1024)S(1)} %pmax.7), kind=kLoop, calls=%fused_computation.7 | loop fusion | flops 90144768 | bytes 77279232 | tf_op jit(solution)/shard_map/convert_element_type | solution.py:122
  834.6 29.7 %fusion.192 = f32[1024,768]{1,0:T(8,128)} fusion(bf16[1024,12576]{0,1:T(8,128)(2,1)} %multiply_convert_fusion, bf16[12576,768]{1,0:T(8,128)(2,1)} %convert_element_type.183), kind=kOutput, calls=%fused_computation.333 | convolution fusion | flops 19780337664 | bytes 48218112 | tf_op jit(solution)/shard_map/dot_general | solution.py:124
  864.4 119.1 %all-reduce.25.cloned.1.call-done = f32[1024,768]{1,0:T(8,128)} async-done(((f32[1024,768]{1,0:T(8,128)}), f32[1024,768]{1,0:T(8,128)}) %all-reduce.25.cloned.1.call-update) | async-done | bytes 3145744 | tf_op jit(solution)/shard_map/psum | solution.py:124
  983.5 4.3 multiply_reduce_fusion.6
  991.2 4.0 fusion.190
  996.3 3.1 fusion.110
  999.6 118.9 %all-reduce.27.cloned.1.call-done = f32[1024,768]{1,0:T(8,128)} async-done(((f32[1024,768]{1,0:T(8,128)}), f32[1024,768]{1,0:T(8,128)}) %all-reduce.27.cloned.1.call-update) | async-done | bytes 3145744 | tf_op jit(solution)/shard_map/psum | solution.py:144
  1118.5 3.6 multiply_reduce_fusion.7
  1127.6 6.7 fusion.96
  1134.3 6.6 fusion.127
  1141.0 19.8 fusion.90
  1160.8 20.1 fusion.87
  1183.1 3.1 fusion.125
  1186.7 118.7 %all-reduce.29.cloned.1.call-done = f32[1024,768]{1,0:T(8,128)} async-done(((f32[1024,768]{1,0:T(8,128)}), f32[1024,768]{1,0:T(8,128)}) %all-reduce.29.cloned.1.call-update) | async-done | bytes 3145744 | tf_op jit(solution)/shard_map/psum | solution.py:161
  1305.4 3.6 multiply_reduce_fusion.8
  1314.7 4.4 fusion.191
  1320.2 3.1 fusion.106
  1325.2 30.6 %fusion.154 = f32[12576,768]{1,0:T(8,128)} fusion(bf16[1024,12576]{0,1:T(8,128)(2,1)} %multiply_convert_fusion, f32[1024,768]{1,0:T(8,128)S(1)} %copy-done.10, f32[768]{0:T(1024)S(1)} %copy-done.149, f32[768]{0:T(1024)S(1)} %get-tuple-element.119, f32[1024]{0:T(1024)S(1)} %fusion.141, f32[1024]{0:T(1024)S(1)} %broadcast_multiply_fusion), kind=kOutput, calls=%fused_computation.304 | convolution fusion | flops 19784269824 | bytes 67549184 | tf_op jit(solution)/shard_map/dot_general | solution.py:123
  1355.8 6.5 convolution_bitcast_fusion
  1362.3 80.1 %all-reduce.31.cloned.1.call-done = f32[1024,768]{1,0:T(8,128)} async-done(((f32[1024,768]{1,0:T(8,128)}), f32[1024,768]{1,0:T(8,128)}) %all-reduce.31.cloned.1.call-update) | async-done | bytes 3145744 | tf_op jit(solution)/shard_map/psum | solution.py:144
  1442.5 3.6 multiply_reduce_fusion.9
  1451.3 7.5 fusion.93
  1458.8 7.6 fusion.126
  1466.4 18.7 fusion.84
  1485.1 18.6 fusion.81
  1506.9 3.1 fusion.124
  1510.7 4.3 convolution_bitcast_fusion.2
  1520.1 2.7 pad_maximum_fusion
  1526.6 2.7 pad_maximum_fusion.1
  1535.6 93.5 %all-reduce.33.cloned.1.call-done = f32[1024,768]{1,0:T(8,128)} async-done(((f32[1024,768]{1,0:T(8,128)}), f32[1024,768]{1,0:T(8,128)}) %all-reduce.33.cloned.1.call-update) | async-done | bytes 3145744 | tf_op jit(solution)/shard_map/psum | solution.py:161
  1629.2 3.8 multiply_reduce_fusion.10
  1639.4 34.0 %scatter_custom_fusion = f32[12576,768]{1,0:T(8,128)} fusion(f32[12576,768]{1,0:T(8,128)} %fusion.154, s32[1024]{0:T(1024)} %bitcast.238, f32[1024,768]{1,0:T(8,128)} %get-tuple-element.183, f32[1024]{0:T(1024)S(1)} %negate_multiply_fusion, f32[]{:T(128)} %constant.58.clone.1, pred[1024]{0:T(1024)(128)(4,1)S(1)} %copy-done.136), kind=kCustom, calls=%fused_computation.94 | custom fusion | flops 2359296 | bytes 41784832 | tf_op jit(solution)/shard_map/scatter-add | solution.py:166
  1677.4 25.4 %all-reduce = (f32[]{:T(128)}, f32[2,3,192]{2,1,0:T(4,128)S(1)}, f32[2,768]{1,0:T(2,128)S(1)}, f32[16,768]{1,0:T(8,128)S(1)}) all-reduce(f32[]{:T(128)} %subtract_reduce_fusion, f32[2,3,192]{2,1,0:T(4,128)S(1)} %pad_maximum_fusion.6, f32[2,768]{1,0:T(2,128)S(1)} %pad_maximum_fusion.7, ...), channel_id=1, replica_groups=mesh['tp'=4,'dp'=8] {'dp'}, use_global_device_ids=true, to_apply=%region_28.29 | all-reduce | flops 14977 | bytes 119816 | tf_op jit(solution)/shard_map/psum | solution.py:188
  1704.7 575.7 %all-reduce.35.cloned.1.call-done = (f32[12576,768]{1,0:T(8,128)}, f32[2,768,576]{1,2,0:T(8,128)}, f32[2,192,768]{2,1,0:T(8,128)}, f32[2,768,768]{2,1,0:T(8,128)}, f32[2,768,768]{2,1,0:T(8,128)}) async-done(((f32[12576,768]{1,0:T(8,128)}, f32[2,768,576]{1,2,0:T(8,128)}, f32[2,192,768]{2,1,0:T(8,128)}, f32[2,768,768]{2,1,0:T(8,128)}, f32[2,768,768]{2,1,0:T(8,128)}), (f32[12576,768]{1,0:T(8,128)}, ...) | async-done | bytes 52789264 | tf_op jit(solution)/shard_map/psum | solution.py:189
  2280.4 19.3 multiply_reduce_fusion
  2310.9 12.4 psum.174
  2327.1 90.3 %fusion.172 = (bf16[12576,768]{1,0:T(8,128)(2,1)}, f32[12576,768]{1,0:T(8,128)}, f32[12576,768]{1,0:T(8,128)}, f32[12576,768]{1,0:T(8,128)}) fusion(f32[12576,768]{1,0:T(8,128)} %param.29, f32[12576,768]{1,0:T(8,128)} %get-tuple-element.143, f32[]{:T(128)S(6)} %min.22, f32[12576,768]{1,0:T(8,128)} %param.37, f32[12576,768]{1,0:T(8,128)} %param.45), kind=kLoop, calls=%fused_computation.314 | loop fusion | flops 164192256 | bytes 289751040 | tf_op jit(solution)/shard_map/convert_element_type | solution.py:197
  2418.2 10.2 fusion.168
  2429.0 2.6 fusion.163
  2432.4 23.2 fusion.157
  (499 shorter events, 116.7 us)
Async XLA Ops:
  7.2 162.9 %all-reduce.15.cloned.1.call-start = ((), (), s32[]{:S(2)}) async-start(), calls=%async_computation | async-start | bytes 6291456 | tf_op jit(solution)/shard_map/psum | solution.py:85
  8.0 21.4 copy-start.134
  8.7 35.2 %copy-start.135 = (pred[1024]{0:T(1024)(128)(4,1)}, pred[1024]{0:T(1024)(128)(4,1)S(1)}, u32[]{:S(2)}) copy-start(pred[1024]{0:T(1024)(128)(4,1)S(1)} %and_reduce_fusion) | copy-start | bytes 3076
  47.3 272.2 %all-reduce.17.cloned.1.call-start = ((), (), s32[]{:S(2)}) async-start(), calls=%async_computation.1 | async-start | bytes 6291456 | tf_op jit(solution)/shard_map/psum | solution.py:100
  52.9 122.6 %copy-start.84 = (f32[768]{0:T(1024)}, f32[768]{0:T(1024)S(1)}, u32[]{:S(2)}) copy-start(f32[768]{0:T(1024)S(1)} %get-tuple-element.131) | copy-start | bytes 9220
  52.9 266.6 %copy-start.72 = (f32[768]{0:T(1024)}, f32[768]{0:T(1024)S(1)}, u32[]{:S(2)}) copy-start(f32[768]{0:T(1024)S(1)} %get-tuple-element.133) | copy-start | bytes 9220
  52.9 266.6 %copy-start.77 = (f32[768]{0:T(1024)}, f32[768]{0:T(1024)S(1)}, u32[]{:S(2)}) copy-start(f32[768]{0:T(1024)S(1)} %get-tuple-element.132) | copy-start | bytes 9220
  52.9 270.1 %copy-start.100 = (f32[768]{0:T(1024)}, f32[768]{0:T(1024)S(1)}, u32[]{:S(2)}) copy-start(f32[768]{0:T(1024)S(1)} %get-tuple-element.128) | copy-start | bytes 9220
  52.9 270.1 %copy-start.141 = (f32[768]{0:T(1024)}, f32[768]{0:T(1024)S(1)}, u32[]{:S(2)}) copy-start(f32[768]{0:T(1024)S(1)} %get-tuple-element.127) | copy-start | bytes 9220
  52.9 402.5 %copy-start.86 = (f32[768]{0:T(1024)}, f32[768]{0:T(1024)S(1)}, u32[]{:S(2)}) copy-start(f32[768]{0:T(1024)S(1)} %get-tuple-element.125) | copy-start | bytes 9220
  52.9 548.5 %copy-start.143 = (f32[768]{0:T(1024)}, f32[768]{0:T(1024)S(1)}, u32[]{:S(2)}) copy-start(f32[768]{0:T(1024)S(1)} %get-tuple-element.121) | copy-start | bytes 9220
  52.9 681.5 %copy-start.148 = (f32[768]{0:T(1024)}, f32[768]{0:T(1024)S(1)}, u32[]{:S(2)}) copy-start(f32[768]{0:T(1024)S(1)} %get-tuple-element.134) | copy-start | bytes 9220
  52.9 1069.2 %copy-start.102 = (f32[768]{0:T(1024)}, f32[768]{0:T(1024)S(1)}, u32[]{:S(2)}) copy-start(f32[768]{0:T(1024)S(1)} %get-tuple-element.122) | copy-start | bytes 9220
  172.9 146.6 %copy-start.70 = (f32[1024]{0:T(1024)}, f32[1024]{0:T(1024)S(1)}, u32[]{:S(2)}) copy-start(f32[1024]{0:T(1024)S(1)} %broadcast_multiply_fusion.5) | copy-start | bytes 12292
  173.4 146.1 %copy-start.74 = (f32[1024]{0:T(1024)}, f32[1024]{0:T(1024)S(1)}, u32[]{:S(2)}) copy-start(f32[1024]{0:T(1024)S(1)} %fusion.136) | copy-start | bytes 12292
  200.4 251.2 %all-reduce.19.cloned.1.call-start = ((), (), s32[]{:S(2)}) async-start(), calls=%async_computation.2 | async-start | bytes 6291456 | tf_op jit(solution)/shard_map/psum | solution.py:107
  219.8 107.1 %copy-start.144 = (f32[768]{0:T(1024)}, f32[768]{0:T(1024)S(1)}, u32[]{:S(2)}) copy-start(f32[768]{0:T(1024)S(1)} %get-tuple-element.136) | copy-start | bytes 9220
  219.9 769.8 %copy-start.150 = (f32[768]{0:T(1024)}, f32[768]{0:T(1024)S(1)}, u32[]{:S(2)}) copy-start(f32[768]{0:T(1024)S(1)} %get-tuple-element.135) | copy-start | bytes 9220
  332.4 266.1 %all-reduce.21.cloned.1.call-start = ((), (), s32[]{:S(2)}) async-start(), calls=%async_computation.3 | async-start | bytes 6291456 | tf_op jit(solution)/shard_map/psum | solution.py:100
  454.8 143.7 %copy-start.2 = (f32[1024,768]{1,0:T(8,128)}, f32[1024,768]{1,0:T(8,128)S(1)}, u32[]{:S(2)}) copy-start(f32[1024,768]{1,0:T(8,128)S(1)} %get-tuple-element.206) | copy-start | bytes 9437188
  479.4 250.5 %all-reduce.23.cloned.1.call-start = ((), (), s32[]{:S(2)}) async-start(), calls=%async_computation.4 | async-start | bytes 6291456 | tf_op jit(solution)/shard_map/psum | solution.py:107
  600.8 521.3 %copy-start.92 = (f32[1024]{0:T(1024)}, f32[1024]{0:T(1024)S(1)}, u32[]{:S(2)}) copy-start(f32[1024]{0:T(1024)S(1)} %broadcast_multiply_fusion.1) | copy-start | bytes 12292
  601.4 520.7 %copy-start.107 = (f32[1024]{0:T(1024)}, f32[1024]{0:T(1024)S(1)}, u32[]{:S(2)}) copy-start(f32[1024]{0:T(1024)S(1)} %fusion.140) | copy-start | bytes 12292
  610.7 119.2 %copy-start.7 = (f32[1024,768]{1,0:T(8,128)S(1)}, f32[1024,768]{1,0:T(8,128)}, u32[]{:S(2)}) copy-start(f32[1024,768]{1,0:T(8,128)} %copy-done.6) | copy-start | bytes 9437188
  610.8 372.7 %all-reduce.25.cloned.1.call-start = ((), (), s32[]{:S(2)}) async-start(), calls=%async_computation.5 | async-start | bytes 6291456 | tf_op jit(solution)/shard_map/psum | solution.py:124
  776.4 31.6 %copy-start.96 = (f32[1024]{0:T(1024)}, f32[1024]{0:T(1024)S(1)}, u32[]{:S(2)}) copy-start(f32[1024]{0:T(1024)S(1)} %pmax.7) | copy-start | bytes 12292
  808.1 26.5 %copy-start.120 = (f32[1024]{0:T(1024)}, f32[1024]{0:T(1024)S(1)}, u32[]{:S(2)}) copy-start(f32[1024]{0:T(1024)S(1)} %get-tuple-element.149) | copy-start | bytes 12292
  864.3 254.2 %all-reduce.27.cloned.1.call-start = ((), (), s32[]{:S(2)}) async-start(), calls=%async_computation.6 | async-start | bytes 6291456 | tf_op jit(solution)/shard_map/psum | solution.py:144
  999.4 306.0 %all-reduce.29.cloned.1.call-start = ((), (), s32[]{:S(2)}) async-start(), calls=%async_computation.7 | async-start | bytes 6291456 | tf_op jit(solution)/shard_map/psum | solution.py:161
  1134.3 46.6 %copy-start.36 = (f32[1,1024,3,1,64]{1,4,2,3,0:T(8,128)}, f32[1,1024,3,1,64]{1,4,2,3,0:T(8,128)S(1)}, u32[]{:S(2)}) copy-start(f32[1,1024,3,1,64]{1,4,2,3,0:T(8,128)S(1)} %fusion.96) | copy-start | bytes 2359300
  1160.8 20.2 copy-start.38
  1183.1 122.3 %copy-start.83 = (f32[1024]{0:T(1024)S(1)}, f32[1024]{0:T(1024)}, u32[]{:S(2)}) copy-start(f32[1024]{0:T(1024)} %copy-done.82) | copy-start | bytes 12292
  1183.1 122.3 %copy-start.87 = (f32[768]{0:T(1024)S(1)}, f32[768]{0:T(1024)}, u32[]{:S(2)}) copy-start(f32[768]{0:T(1024)} %copy-done.86) | copy-start | bytes 9220
  1183.1 122.3 %copy-start.95 = (f32[1024]{0:T(1024)S(1)}, f32[1024]{0:T(1024)}, u32[]{:S(2)}) copy-start(f32[1024]{0:T(1024)} %copy-done.94) | copy-start | bytes 12292
  1186.2 119.2 %copy-start.3 = (f32[1024,768]{1,0:T(8,128)S(1)}, f32[1024,768]{1,0:T(8,128)}, u32[]{:S(2)}) copy-start(f32[1024,768]{1,0:T(8,128)} %copy-done.2) | copy-start | bytes 9437188
  1186.3 122.7 %copy-start.115 = (f32[1024]{0:T(1024)S(1)}, f32[1024]{0:T(1024)}, u32[]{:S(2)}) copy-start(f32[1024]{0:T(1024)} %copy-done.114) | copy-start | bytes 12292
  1186.3 256.2 %all-reduce.31.cloned.1.call-start = ((), (), s32[]{:S(2)}) async-start(), calls=%async_computation.8 | async-start | bytes 6291456 | tf_op jit(solution)/shard_map/psum | solution.py:144
  1323.3 32.5 %copy-start.151 = (f32[768]{0:T(1024)S(1)}, f32[768]{0:T(1024)}, u32[]{:S(2)}) copy-start(f32[768]{0:T(1024)} %copy-done.150) | copy-start | bytes 9220
  1323.3 305.8 %all-reduce.33.cloned.1.call-start = ((), (), s32[]{:S(2)}) async-start(), calls=%async_computation.9 | async-start | bytes 6291456 | tf_op jit(solution)/shard_map/psum | solution.py:161
  1355.8 86.6 %copy-start.5 = (f32[1024,768]{1,0:T(8,128)S(1)}, f32[1024,768]{1,0:T(8,128)}, u32[]{:S(2)}) copy-start(f32[1024,768]{1,0:T(8,128)} %copy-done.4) | copy-start | bytes 9437188
  1355.8 86.6 %copy-start.91 = (f32[1024]{0:T(1024)S(1)}, f32[1024]{0:T(1024)}, u32[]{:S(2)}) copy-start(f32[1024]{0:T(1024)} %copy-done.90) | copy-start | bytes 12292
  1355.8 86.6 %copy-start.101 = (f32[768]{0:T(1024)S(1)}, f32[768]{0:T(1024)}, u32[]{:S(2)}) copy-start(f32[768]{0:T(1024)} %copy-done.100) | copy-start | bytes 9220
  1355.8 86.6 %copy-start.105 = (f32[1024]{0:T(1024)S(1)}, f32[1024]{0:T(1024)}, u32[]{:S(2)}) copy-start(f32[1024]{0:T(1024)} %copy-done.104) | copy-start | bytes 12292
  1362.3 83.7 %copy-start.113 = (f32[1024]{0:T(1024)S(1)}, f32[1024]{0:T(1024)}, u32[]{:S(2)}) copy-start(f32[1024]{0:T(1024)} %copy-done.112) | copy-start | bytes 12292
  1510.0 770.4 %all-reduce.35.cloned.1.call-start = ((), (), s32[]{:S(2)}) async-start(), calls=%async_computation.10 | async-start | bytes 105578496 | tf_op jit(solution)/shard_map/psum | solution.py:189
  1533.5 95.6 %copy-start.1 = (f32[1024,768]{1,0:T(8,128)S(1)}, f32[1024,768]{1,0:T(8,128)}, u32[]{:S(2)}) copy-start(f32[1024,768]{1,0:T(8,128)} %all-reduce.15.cloned.1.call-done) | copy-start | bytes 9437188
  1533.5 95.6 %copy-start.71 = (f32[1024]{0:T(1024)S(1)}, f32[1024]{0:T(1024)}, u32[]{:S(2)}) copy-start(f32[1024]{0:T(1024)} %copy-done.70) | copy-start | bytes 12292
  1533.5 95.6 %copy-start.73 = (f32[768]{0:T(1024)S(1)}, f32[768]{0:T(1024)}, u32[]{:S(2)}) copy-start(f32[768]{0:T(1024)} %copy-done.72) | copy-start | bytes 9220
  1533.5 95.6 %copy-start.75 = (f32[1024]{0:T(1024)S(1)}, f32[1024]{0:T(1024)}, u32[]{:S(2)}) copy-start(f32[1024]{0:T(1024)} %copy-done.74) | copy-start | bytes 12292
  1533.5 95.6 %copy-start.78 = (f32[768]{0:T(1024)S(1)}, f32[768]{0:T(1024)}, u32[]{:S(2)}) copy-start(f32[768]{0:T(1024)} %copy-done.77) | copy-start | bytes 9220
  1533.6 95.6 %copy-start.81 = (f32[1024]{0:T(1024)S(1)}, f32[1024]{0:T(1024)}, u32[]{:S(2)}) copy-start(f32[1024]{0:T(1024)} %copy-done.80) | copy-start | bytes 12292
  1533.6 95.6 %copy-start.85 = (f32[768]{0:T(1024)S(1)}, f32[768]{0:T(1024)}, u32[]{:S(2)}) copy-start(f32[768]{0:T(1024)} %copy-done.84) | copy-start | bytes 9220
  1533.6 95.6 %copy-start.89 = (f32[1024]{0:T(1024)S(1)}, f32[1024]{0:T(1024)}, u32[]{:S(2)}) copy-start(f32[1024]{0:T(1024)} %copy-done.88) | copy-start | bytes 12292
  1535.6 97.4 %copy-start.111 = (f32[1024]{0:T(1024)S(1)}, f32[1024]{0:T(1024)}, u32[]{:S(2)}) copy-start(f32[1024]{0:T(1024)} %copy-done.110) | copy-start | bytes 12292
  2280.4 21.7 slice-start.4
  2280.4 23.5 slice-start.6
  2280.4 21.7 slice-start.5
  2280.4 23.5 slice-start.7
  2303.9 20.8 copy-start.117
  2303.9 20.8 copy-start.137
  2303.9 20.8 copy-start.138
  2327.1 90.3 %copy-start.79 = (f32[16,768]{1,0:T(8,128)S(1)}, f32[16,768]{1,0:T(8,128)}, u32[]{:S(2)}) copy-start(f32[16,768]{1,0:T(8,128)} %param.30) | copy-start | bytes 147460
  2327.1 90.3 %copy-start.98 = (f32[16,768]{1,0:T(8,128)S(1)}, f32[16,768]{1,0:T(8,128)}, u32[]{:S(2)}) copy-start(f32[16,768]{1,0:T(8,128)} %param.38) | copy-start | bytes 147460
  2327.1 90.3 %copy-start.99 = (f32[16,768]{1,0:T(8,128)S(1)}, f32[16,768]{1,0:T(8,128)}, u32[]{:S(2)}) copy-start(f32[16,768]{1,0:T(8,128)} %param.46) | copy-start | bytes 147460
  (123 other events, 432.5 us)
Sparse Core Ops, SparseCore 0:
  47.4 122.6 all-reduce.14
  200.5 118.9 all-reduce.16
  332.5 118.9 all-reduce.18
  479.5 118.9 all-reduce.20
  610.9 118.9 all-reduce.22
  864.4 118.9 all-reduce.24
  999.5 118.9 all-reduce.26
  1186.4 118.9 all-reduce.28
  1323.4 118.9 all-reduce.30
  1510.1 118.9 all-reduce.32
  1673.7 606.6 all-reduce.34
where the time goes:
time: 2470 us; the launch traced here: 2460 us
  waiting for transfers between devices  1680 us (68%)
  other arithmetic  346 us (14%)
  matrix products  291 us (12%)
  blocking collectives  57.2 us (2%)
  local copies, waits for them, and re-layouts  56 us (2%)
    psum x1, waiting for transfers between devices, device_step(): grads = [lax.psum(grad_arr, 'dp') for grad_arr in grads]  576 us
    psum x2, waiting for transfers between devices, local_grads(): lax.psum(jnp.dot(hidden, wdown_b[layer], preferred_element_type=jnp.float...  238 us
    psum x2, waiting for transfers between devices, local_grads(): lax.psum(jnp.dot(context, wout_b[layer], preferred_element_type=jnp.float...  219 us
    psum x2, waiting for transfers between devices, local_grads(): lax.psum(lax.dot_general(d_qkv_b, wqkv_b[layer], CONTRACT_COLS, preferred...  212 us
    psum x2, waiting for transfers between devices, local_grads(): lax.psum(lax.dot_general(d_pre_b, wup_b[layer], CONTRACT_COLS, preferred_...  199 us
    convert_element_type x7, other arithmetic, device_step(): new_bf16 = [entry.astype(jnp.bfloat16) for entry in new_masters]  128 us
    psum x1, waiting for transfers between devices, local_grads(): lax.psum(jnp.dot(d_logits, emb_b, preferred_element_type=jnp.float32), 'tp')  119 us
    psum x1, waiting for transfers between devices, local_grads(): lax.psum(jnp.where(in_shard[:, None], picked.astype(jnp.float32), 0.0), '...  113 us
  transfers between devices with their start and end apart: 11, of which 11 were waited for; matrix products, arithmetic and copies ran while one was open for 3% of the time, Pallas kernels for 0%

commit v1 on v0

v1 whole, which is shorter than its diff:
```python
import functools
import math
import jax
import jax.numpy as jnp
from jax import lax
from jax.experimental import pallas as pl
from jax.experimental.pallas import tpu as pltpu
from jax.sharding import PartitionSpec as P

LN_EPS = 1e-5
CLIP_NORM = 1.0
BETA_ONE = 0.9
BETA_TWO = 0.95
ADAM_EPS = 1e-8
WEIGHT_DECAY = 0.1
LEARN_RATE = 1e-3
STEP_COUNT = 10
DECAYED = (True, False, True, False, True, True, False, True)
PARAM_SPECS = (P('tp', None), P(None, None), P(None, None, 'tp'), P(None, 'tp', None), P(None, 'tp', None), P(None, None, 'tp'), P(None, 'tp'), P(None, 'tp', None))
CONTRACT_ROWS = (((0,), (0,)), ((), ()))
CONTRACT_COLS = (((1,), (1,)), ((), ()))
F32 = jnp.float32
BF16 = jnp.bfloat16
ALL = ('tp', 'dp')
TP = 4
DP = 8
D = 768
SEQ = 1024
HEAD = 64
HEADS_LOC = 3
QW = HEADS_LOC * HEAD
QP = 256
FF_LOC = 768
LAYERS = 2
VOCAB_LOC = 12576
PIECE = 1576
PIECE_PAD = 1664
NTOK = 8192
QUART = 256
ATT_BLK = 256
HEAD_TILE = 512
NEG = -1e30
ROWS_QKV = 72
ROWS_OUT = 24
ROWS_FF = 96
PACK = 296


def alibi_slopes(heads):
    closest = 2 ** int(math.floor(math.log2(heads)))
    first_base = 2.0 ** (-8.0 / closest)
    slopes = [first_base ** (head_idx + 1) for head_idx in range(closest)]
    extra_base = 2.0 ** (-4.0 / closest)
    extra_count = min(closest, heads - closest)
    return slopes + [extra_base ** (2 * head_idx + 1) for head_idx in range(extra_count)]


def layer_norm(values, gain, bias):
    return normalise(values) * gain + bias


def normalise(values):
    centred = values - jnp.mean(values, axis=-1, keepdims=True)
    variance = jnp.mean(centred * centred, axis=-1, keepdims=True)
    return centred * lax.rsqrt(variance + LN_EPS)


def gelu_tanh(values):
    return jax.nn.gelu(values, approximate=True)


def adam_update(master, grad_arr, moment, velocity, decayed):
    mom_new = BETA_ONE * moment + (1.0 - BETA_ONE) * grad_arr
    vel_new = BETA_TWO * velocity + (1.0 - BETA_TWO) * grad_arr * grad_arr
    mom_hat = mom_new / (1.0 - BETA_ONE ** STEP_COUNT)
    vel_hat = vel_new / (1.0 - BETA_TWO ** STEP_COUNT)
    direction = mom_hat / (jnp.sqrt(vel_hat) + ADAM_EPS)
    if decayed:
        direction = direction + WEIGHT_DECAY * master
    return master - LEARN_RATE * direction, mom_new, vel_new


def dot(lhs, rhs, dims=(((1,), (0,)), ((), ()))):
    return lax.dot_general(lhs, rhs, dims, preferred_element_type=F32)


def unpack_kernel(which_ref, full_ref, qkv_ref, up_ref, down_ref, out_ref, bias_ref):
    del which_ref
    pairs = DP // 2
    up_at = ROWS_QKV
    down_at = up_at + ROWS_FF
    out_at = down_at + ROWS_FF
    bias_at = out_at + ROWS_OUT
    for pair in range(pairs):
        rows = pl.ds(2 * ROWS_OUT * pair, 2 * ROWS_OUT)
        for part in range(3):
            at = pl.ds(part * ROWS_OUT, ROWS_OUT)
            both = jnp.concatenate([full_ref[2 * pair, at, :], full_ref[2 * pair + 1, at, :]], axis=0)
            qkv_ref[0, part, rows, :] = both.astype(BF16)
        at = pl.ds(out_at, ROWS_OUT)
        both = jnp.concatenate([full_ref[2 * pair, at, :], full_ref[2 * pair + 1, at, :]], axis=0)
        out_ref[0, rows, :] = both.astype(BF16)
    zero = jnp.zeros((QP - QW, D), BF16)
    for part in range(3):
        qkv_ref[0, part, QW:, :] = zero
    out_ref[0, QW:, :] = zero
    for piece in range(DP):
        rows = pl.ds(ROWS_FF * piece, ROWS_FF)
        up_ref[rows, :] = full_ref[piece, pl.ds(up_at, ROWS_FF), :].astype(BF16)
        down_ref[rows, :] = full_ref[piece, pl.ds(down_at, ROWS_FF), :].astype(BF16)
    bias_ref[0] = full_ref[0, pl.ds(bias_at, 8), :]


def unpack_weights(full, core):
    grid_spec = pltpu.PrefetchScalarGridSpec(
        num_scalar_prefetch=1,
        grid=(2,),
        in_specs=[pl.BlockSpec((DP, PACK, D), lambda s, which: (2 * which[0] + s, 0, 0))],
        out_specs=[
            pl.BlockSpec((1, 3, QP, D), lambda s, which: (s, 0, 0, 0)),
            pl.BlockSpec((D, FF_LOC), lambda s, which: (0, s)),
            pl.BlockSpec((FF_LOC, D), lambda s, which: (s, 0)),
            pl.BlockSpec((1, QP, D), lambda s, which: (s, 0, 0)),
            pl.BlockSpec((1, 8, D), lambda s, which: (s, 0, 0)),
        ],
    )
    shapes = [
        jax.ShapeDtypeStruct((2, 3, QP, D), BF16),
        jax.ShapeDtypeStruct((D, 2 * FF_LOC), BF16),
        jax.ShapeDtypeStruct((2 * FF_LOC, D), BF16),
        jax.ShapeDtypeStruct((2, QP, D), BF16),
        jax.ShapeDtypeStruct((2, 8, D), F32),
    ]
    qkv, up, down, out, bias = pl.pallas_call(
        unpack_kernel,
        out_shape=shapes,
        grid_spec=grid_spec,
        compiler_params=pltpu.CompilerParams(vmem_limit_bytes=40 << 20),
        cost_estimate=pl.CostEstimate(flops=8 * 2368 * D * 2, bytes_accessed=22 << 20, transcendentals=0),
        name='unpack_weights',
    )(core.reshape(1), full)
    return qkv.reshape(2 * 3 * QP, D), up, down, out.reshape(2 * QP, D), bias


def pack_weights(w_qkv, b_qkv, w_out, w_up, b_up, w_down, dp_rank):
    qkv_t = w_qkv.T.reshape(HEADS_LOC, 3, HEAD, D).transpose(1, 0, 2, 3).reshape(3, QW, D)
    qkv_piece = lax.dynamic_slice(qkv_t, (0, dp_rank * ROWS_OUT, 0), (3, ROWS_OUT, D)).reshape(ROWS_QKV, D)
    up_piece = lax.dynamic_slice(w_up, (dp_rank * ROWS_FF, 0), (ROWS_FF, FF_LOC))
    down_piece = lax.dynamic_slice(w_down, (dp_rank * ROWS_FF, 0), (ROWS_FF, D))
    out_piece = lax.dynamic_slice(w_out, (dp_rank * ROWS_OUT, 0), (ROWS_OUT, D))
    b_row = b_qkv.reshape(HEADS_LOC, 3, HEAD).transpose(1, 0, 2).reshape(3, QW)
    b_row = jnp.pad(b_row, ((0, 0), (0, QP - QW))).reshape(1, D)
    bias = jnp.concatenate([b_row, b_up.reshape(1, FF_LOC), jnp.zeros((6, D), F32)], axis=0)
    return jnp.concatenate([qkv_piece, up_piece, down_piece, out_piece, bias], axis=0)


def head_masks(rows):
    lane = lax.broadcasted_iota(jnp.int32, (rows, QP), 1)
    return [(lane >= HEAD * j) & (lane < HEAD * (j + 1)) for j in range(HEADS_LOC)]


def block_probs(query, keys, slope, row0, width):
    scores = dot(query, keys, CONTRACT_COLS) * (HEAD ** -0.5)
    row = lax.broadcasted_iota(jnp.int32, (ATT_BLK, width), 0) + row0
    col = lax.broadcasted_iota(jnp.int32, (ATT_BLK, width), 1)
    rel = col - row
    scores = scores + slope * rel.astype(F32)
    scores = jnp.where(rel <= 0, scores, NEG)
    top = jnp.max(scores, axis=1, keepdims=True)
    shifted = jnp.exp(scores - top)
    return shifted * (1.0 / jnp.sum(shifted, axis=1, keepdims=True))


def attn_fwd_kernel(slope_ref, qkv_ref, ctx_ref):
    group = pl.program_id(0)
    masks = head_masks(ATT_BLK)
    for blk in range(SEQ // ATT_BLK):
        row0 = blk * ATT_BLK
        width = row0 + ATT_BLK
        query = qkv_ref[row0:width, 0:QP]
        keys = qkv_ref[0:width, QP:2 * QP]
        values = qkv_ref[0:width, 2 * QP:3 * QP]
        ctx = jnp.zeros((ATT_BLK, QP), F32)
        for j in range(HEADS_LOC):
            slope = slope_ref[group * HEADS_LOC + j]
            probs = block_probs(jnp.where(masks[j], query, 0).astype(BF16), keys, slope, row0, width)
            ctx = jnp.where(masks[j], dot(probs.astype(BF16), values), ctx)
        ctx_ref[row0:width, :] = ctx.astype(BF16)


def attn_bwd_kernel(slope_ref, qkv_ref, dctx_ref, dqkv_ref, dbias_ref, dk_ref, dv_ref):
    group = pl.program_id(0)
    masks = head_masks(ATT_BLK)
    dk_ref[...] = jnp.zeros_like(dk_ref)
    dv_ref[...] = jnp.zeros_like(dv_ref)
    dq_sum = jnp.zeros((1, QP), F32)
    for blk in range(SEQ // ATT_BLK):
        row0 = blk * ATT_BLK
        width = row0 + ATT_BLK
        query = qkv_ref[row0:width, 0:QP]
        keys = qkv_ref[0:width, QP:2 * QP]
        values = qkv_ref[0:width, 2 * QP:3 * QP]
        dctx = dctx_ref[row0:width, :]
        dq = jnp.zeros((ATT_BLK, QP), F32)
        for j in range(HEADS_LOC):
            slope = slope_ref[group * HEADS_LOC + j]
            q_one = jnp.where(masks[j], query, 0).astype(BF16)
            dc_one = jnp.where(masks[j], dctx, 0).astype(BF16)
            probs = block_probs(q_one, keys, slope, row0, width)
            d_probs = dot(dc_one, values, CONTRACT_COLS)
            inner = jnp.sum(probs * d_probs, axis=1, keepdims=True)
            d_scores = (probs * (d_probs - inner) * (HEAD ** -0.5)).astype(BF16)
            dv_ref[0:width, :] += dot(probs.astype(BF16), dc_one, CONTRACT_ROWS)
            dk_ref[0:width, :] += dot(d_scores, q_one, CONTRACT_ROWS)
            dq = jnp.where(masks[j], dot(d_scores, keys), dq)
        dqkv_ref[row0:width, 0:QP] = dq.astype(BF16)
        dq_sum = dq_sum + jnp.sum(dq, axis=0, keepdims=True)
    dqkv_ref[:, QP:2 * QP] = dk_ref[...].astype(BF16)
    dqkv_ref[:, 2 * QP:3 * QP] = dv_ref[...].astype(BF16)
    dbias_ref[0, :, 0:QP] = jnp.broadcast_to(dq_sum, (8, QP))
    dbias_ref[0, :, QP:2 * QP] = jnp.broadcast_to(jnp.sum(dk_ref[...], axis=0, keepdims=True), (8, QP))
    dbias_ref[0, :, 2 * QP:3 * QP] = jnp.broadcast_to(jnp.sum(dv_ref[...], axis=0, keepdims=True), (8, QP))


def attn_fwd(qkv, slopes):
    return pl.pallas_call(
        attn_fwd_kernel,
        grid=(2,),
        out_shape=jax.ShapeDtypeStruct((SEQ, 2 * QP), BF16),
        in_specs=[pl.BlockSpec(memory_space=pltpu.SMEM), pl.BlockSpec((SEQ, 3 * QP), lambda g: (0, g))],
        out_specs=pl.BlockSpec((SEQ, QP), lambda g: (0, g)),
        compiler_params=pltpu.CompilerParams(vmem_limit_bytes=40 << 20),
        cost_estimate=pl.CostEstimate(flops=10 * 1000 * 1000 * 1000, bytes_accessed=4 << 20, transcendentals=4 << 20),
        name='attn_fwd',
    )(slopes, qkv)


def attn_bwd(qkv, dctx, slopes):
    return pl.pallas_call(
        attn_bwd_kernel,
        grid=(2,),
        out_shape=[jax.ShapeDtypeStruct((SEQ, 6 * QP), BF16), jax.ShapeDtypeStruct((2, 8, 3 * QP), F32)],
        in_specs=[
            pl.BlockSpec(memory_space=pltpu.SMEM),
            pl.BlockSpec((SEQ, 3 * QP), lambda g: (0, g)),
            pl.BlockSpec((SEQ, QP), lambda g: (0, g)),
        ],
        out_specs=[pl.BlockSpec((SEQ, 3 * QP), lambda g: (0, g)), pl.BlockSpec((1, 8, 3 * QP), lambda g: (g, 0, 0))],
        scratch_shapes=[pltpu.VMEM((SEQ, QP), F32), pltpu.VMEM((SEQ, QP), F32)],
        compiler_params=pltpu.CompilerParams(vmem_limit_bytes=40 << 20),
        cost_estimate=pl.CostEstimate(flops=25 * 1000 * 1000 * 1000, bytes_accessed=8 << 20, transcendentals=4 << 20),
        name='attn_bwd',
    )(slopes, qkv, dctx)


ROW_CHUNK = 128
CHUNKS = PIECE_PAD // ROW_CHUNK


def head_fwd_kernel(valid_ref, xhat_ref, gain_ref, bias_ref, emb_ref, lab_ref, head_ref, logit_ref, stat_ref):
    head_in = (xhat_ref[...] * gain_ref[...] + bias_ref[...]).astype(BF16)
    head_ref[...] = head_in
    valid = valid_ref[0]
    top = jnp.full((1, HEAD_TILE), NEG, F32)
    for chunk in range(CHUNKS):
        rows = slice(chunk * ROW_CHUNK, (chunk + 1) * ROW_CHUNK)
        part = dot(emb_ref[rows, :], head_in, CONTRACT_COLS)
        if (chunk + 1) * ROW_CHUNK > PIECE - 32:
            row = lax.broadcasted_iota(jnp.int32, part.shape, 0) + chunk * ROW_CHUNK
            part = jnp.where(row < valid, part, NEG)
        logit_ref[rows, :] = part
        top = jnp.maximum(top, jnp.max(part, axis=0, keepdims=True))
    total = jnp.zeros((1, HEAD_TILE), F32)
    target = jnp.zeros((1, HEAD_TILE), F32)
    label = lab_ref[...]
    for chunk in range(CHUNKS):
        rows = slice(chunk * ROW_CHUNK, (chunk + 1) * ROW_CHUNK)
        part = logit_ref[rows, :]
        row = lax.broadcasted_iota(jnp.int32, part.shape, 0) + chunk * ROW_CHUNK
        total = total + jnp.sum(jnp.exp(part - top), axis=0, keepdims=True)
        target = target + jnp.sum(jnp.where(row == label, part, 0.0), axis=0, keepdims=True)
    stat_ref[0:1, :] = top
    stat_ref[1:2, :] = total
    stat_ref[2:3, :] = target
    stat_ref[3:8, :] = jnp.zeros((5, HEAD_TILE), F32)


def head_bwd_kernel(logit_ref, head_ref, emb_ref, lab_ref, stat_ref, dhead_ref, gemb_ref):
    @pl.when(pl.program_id(0) == 0)
    def _():
        gemb_ref[...] = jnp.zeros_like(gemb_ref)

    top = stat_ref[0:1, :]
    inverse = 1.0 / stat_ref[1:2, :]
    label = lab_ref[...]
    head_in = head_ref[...]
    dhead = jnp.zeros((HEAD_TILE, D), F32)
    for chunk in range(CHUNKS):
        rows = slice(chunk * ROW_CHUNK, (chunk + 1) * ROW_CHUNK)
        part = logit_ref[rows, :]
        row = lax.broadcasted_iota(jnp.int32, part.shape, 0) + chunk * ROW_CHUNK
        soft = jnp.exp(part - top) * inverse
        d_logit = ((soft - jnp.where(row == label, 1.0, 0.0)) * (1.0 / NTOK)).astype(BF16)
        gemb_ref[rows, :] += dot(d_logit, head_in)
        dhead = dhead + dot(d_logit, emb_ref[rows, :], CONTRACT_ROWS)
    dhead_ref[...] = dhead


def head_fwd(xhat, gain, bias, emb_piece, label_row, valid):
    return pl.pallas_call(
        head_fwd_kernel,
        grid=(NTOK // HEAD_TILE,),
        out_shape=[
            jax.ShapeDtypeStruct((NTOK, D), BF16),
            jax.ShapeDtypeStruct((PIECE_PAD, NTOK), F32),
            jax.ShapeDtypeStruct((8, NTOK), F32),
        ],
        in_specs=[
            pl.BlockSpec(memory_space=pltpu.SMEM),
            pl.BlockSpec((HEAD_TILE, D), lambda t: (t, 0)),
            pl.BlockSpec((1, D), lambda t: (0, 0)),
            pl.BlockSpec((1, D), lambda t: (0, 0)),
            pl.BlockSpec((PIECE_PAD, D), lambda t: (0, 0)),
            pl.BlockSpec((1, HEAD_TILE), lambda t: (0, t)),
        ],
        out_specs=[
            pl.BlockSpec((HEAD_TILE, D), lambda t: (t, 0)),
            pl.BlockSpec((PIECE_PAD, HEAD_TILE), lambda t: (0, t)),
            pl.BlockSpec((8, HEAD_TILE), lambda t: (0, t)),
        ],
        compiler_params=pltpu.CompilerParams(vmem_limit_bytes=48 << 20),
        cost_estimate=pl.CostEstimate(flops=2 * NTOK * PIECE_PAD * D, bytes_accessed=96 << 20, transcendentals=NTOK * PIECE_PAD),
        name='head_fwd',
    )(valid.reshape(1), xhat, gain, bias, emb_piece, label_row)


def head_bwd(logits, head_in, emb_piece, label_row, stats):
    return pl.pallas_call(
        head_bwd_kernel,
        grid=(NTOK // HEAD_TILE,),
        out_shape=[jax.ShapeDtypeStruct((NTOK, D), F32), jax.ShapeDtypeStruct((PIECE_PAD, D), F32)],
        in_specs=[
            pl.BlockSpec((PIECE_PAD, HEAD_TILE), lambda t: (0, t)),
            pl.BlockSpec((HEAD_TILE, D), lambda t: (t, 0)),
            pl.BlockSpec((PIECE_PAD, D), lambda t: (0, 0)),
            pl.BlockSpec((1, HEAD_TILE), lambda t: (0, t)),
            pl.BlockSpec((8, HEAD_TILE), lambda t: (0, t)),
        ],
        out_specs=[pl.BlockSpec((HEAD_TILE, D), lambda t: (t, 0)), pl.BlockSpec((PIECE_PAD, D), lambda t: (0, 0))],
        compiler_params=pltpu.CompilerParams(vmem_limit_bytes=48 << 20),
        cost_estimate=pl.CostEstimate(flops=4 * NTOK * PIECE_PAD * D, bytes_accessed=96 << 20, transcendentals=NTOK * PIECE_PAD),
        name='head_bwd',
    )(logits, head_in, emb_piece, label_row, stats)


def partner_core(values):
    return lax.ppermute(values, 'dp', [(rank, rank ^ 1) for rank in range(DP)])


def line_pairs(flip):
    return [(z * DP + rank, (z ^ flip) * DP + rank) for z in range(TP) for rank in range(DP)]


def join_core(partial):
    return partial + partner_core(partial)


def device_step(tokens, labels, *state):
    masters = state[0:8]
    moms = state[8:16]
    vels = state[16:24]
    embedding, vec_params, w_qkv, b_qkv, w_out, w_up, b_up, w_down = masters
    z_rank = lax.axis_index('tp')
    dp_rank = lax.axis_index('dp')
    core = dp_rank % 2
    parity = z_rank % 2
    high = z_rank // 2
    quarter = high * 2 + core
    own_shard = parity
    is_holder = core == high

    slope_all = jnp.array(alibi_slopes(HEADS_LOC * TP), dtype=F32)
    slopes = lax.dynamic_slice_in_dim(slope_all, core * 2 * HEADS_LOC, 2 * HEADS_LOC)

    id_local = tokens.reshape(-1) - z_rank * VOCAB_LOC
    in_shard = (id_local >= 0) & (id_local < VOCAB_LOC)
    safe_ids = jnp.clip(id_local, 0, VOCAB_LOC - 1)
    picked = lax.reduce_precision(jnp.take(embedding, safe_ids, axis=0), 8, 7)
    x_own = lax.psum(jnp.where(in_shard[:, None], picked, 0.0), 'tp')

    full = [lax.all_gather(pack_weights(w_qkv[l], b_qkv[l], w_out[l], w_up[l], b_up[l], w_down[l], dp_rank), ALL) for l in range(LAYERS)]
    ids_all = lax.all_gather(jnp.concatenate([tokens, labels], axis=0), 'dp')

    pairs = [(z * DP + 2 * k + z % 2, z * DP + 2 * k + 1 - z % 2) for z in range(TP) for k in range(DP // 2)]
    x_other = lax.ppermute(x_own, ALL, pairs)
    x_embed = jnp.where(core == parity, x_own, x_other)
    resid, ln_zero_vjp = jax.vjp(layer_norm, x_embed, vec_params[0], vec_params[1])

    weights = []
    saved = []
    for layer in range(LAYERS):
        row_base = 2 + 6 * layer
        qkv_w, up_w, down_w, out_w, biases = unpack_weights(full[layer], core)
        normed_one, ln_one_vjp = jax.vjp(layer_norm, resid, vec_params[row_base], vec_params[row_base + 1])
        act_in = normed_one.astype(BF16)
        qkv = (dot(act_in, qkv_w, CONTRACT_COLS) + biases[:, 0].reshape(-1)).astype(BF16)
        context = attn_fwd(qkv, slopes)
        mid = resid + join_core(dot(context, out_w)) + vec_params[row_base + 2]
        normed_two, ln_two_vjp = jax.vjp(layer_norm, mid, vec_params[row_base + 3], vec_params[row_base + 4])
        mlp_in = normed_two.astype(BF16)
        pre_act = dot(mlp_in, up_w) + biases[:, 1].reshape(-1)
        act_out, gelu_vjp = jax.vjp(gelu_tanh, pre_act)
        hidden = act_out.astype(BF16)
        resid = mid + join_core(dot(hidden, down_w)) + vec_params[row_base + 5]
        weights.append((qkv_w, up_w, down_w, out_w))
        saved.append((ln_one_vjp, act_in, qkv, context, ln_two_vjp, mlp_in, gelu_vjp, hidden))

    final_row = 2 + 6 * LAYERS
    normed_fin, ln_fin_vjp = jax.vjp(layer_norm, resid, vec_params[final_row], vec_params[final_row + 1])
    del normed_fin
    xhat = lax.dynamic_slice_in_dim(normalise(resid), quarter * QUART, QUART)
    xhat_all = lax.all_gather(xhat, ALL, tiled=True)

    def gathered_order(ids):
        return ids.reshape(DP // 2, 2, 2, 2, QUART).transpose(2, 1, 0, 3, 4).reshape(-1)

    token_all = gathered_order(ids_all[:, 0])
    label_all = gathered_order(ids_all[:, 1])
    valid = jnp.minimum(PIECE, VOCAB_LOC - dp_rank * PIECE)
    piece_start = jnp.minimum(dp_rank * PIECE, VOCAB_LOC - PIECE)
    emb_piece = lax.dynamic_slice_in_dim(embedding, piece_start, PIECE).astype(BF16)
    over = DP * PIECE - VOCAB_LOC
    emb_piece = jnp.where(dp_rank == DP - 1, jnp.roll(emb_piece, -over, axis=0), emb_piece)
    emb_piece = jnp.pad(emb_piece, ((0, PIECE_PAD - PIECE), (0, 0)))
    label_row = (label_all - z_rank * VOCAB_LOC - dp_rank * PIECE)
    label_row = jnp.where(label_row < valid, label_row, -1).reshape(1, NTOK)
    head_in, logits, stat_loc = head_fwd(xhat_all, vec_params[final_row:final_row + 1], vec_params[final_row + 1:final_row + 2], emb_piece, label_row, valid)
    glob_max = lax.pmax(stat_loc[0], ALL)
    sums = lax.psum(jnp.stack([stat_loc[1] * jnp.exp(stat_loc[0] - glob_max), stat_loc[2]]), ALL)
    loss = jnp.sum(glob_max + jnp.log(sums[0]) - sums[1]) / NTOK
    stats = jnp.concatenate([glob_max[None], sums[0:1], jnp.zeros((6, NTOK), F32)], axis=0)
    d_head_part, g_piece = head_bwd(logits, head_in, emb_piece, label_row, stats)
    d_quart = lax.psum_scatter(d_head_part, ALL, scatter_dimension=0, tiled=True)
    d_far = lax.ppermute(d_quart, ALL, line_pairs(2))
    mine = jnp.where(high == 0, jnp.stack([d_quart, d_far]), jnp.stack([d_far, d_quart]))
    theirs = partner_core(mine)
    d_head = jnp.where(core == 0, jnp.stack([mine, theirs], axis=1), jnp.stack([theirs, mine], axis=1)).reshape(SEQ, D)
    g_head = lax.all_gather(g_piece[:PIECE], 'dp', tiled=True)

    vec_grads = {}
    d_resid, vec_grads[final_row], vec_grads[final_row + 1] = ln_fin_vjp(d_head)
    layer_grads = {}
    bias_grads = {}
    for layer in reversed(range(LAYERS)):
        ln_one_vjp, act_in, qkv, context, ln_two_vjp, mlp_in, gelu_vjp, hidden = saved[layer]
        qkv_w, up_w, down_w, out_w = weights[layer]
        row_base = 2 + 6 * layer
        vec_grads[row_base + 5] = jnp.sum(d_resid, axis=0)
        d_out = d_resid.astype(BF16)
        d_hidden = dot(d_out, down_w, CONTRACT_COLS)
        d_pre = gelu_vjp(d_hidden)[0]
        g_bup = jnp.sum(d_pre, axis=0)
        d_pre_b = d_pre.astype(BF16)
        d_norm_two = join_core(dot(d_pre_b, up_w, CONTRACT_COLS))
        d_mid_ln, vec_grads[row_base + 3], vec_grads[row_base + 4] = ln_two_vjp(d_norm_two)
        d_mid = d_resid + d_mid_ln
        vec_grads[row_base + 2] = jnp.sum(d_mid, axis=0)
        d_attn = d_mid.astype(BF16)
        d_context = dot(d_attn, out_w, CONTRACT_COLS).astype(BF16)
        d_qkv, g_bqkv = attn_bwd(qkv, d_context, slopes)
        d_norm_one = join_core(dot(d_qkv, qkv_w))
        d_res_ln, vec_grads[row_base], vec_grads[row_base + 1] = ln_one_vjp(d_norm_one)
        d_resid = d_mid + d_res_ln
        bias_grads[layer] = jnp.stack([g_bqkv[:, 0], g_bup.reshape(2, FF_LOC)], axis=1)

        def weight_grads(shard):
            d_pre_s = lax.dynamic_slice_in_dim(d_pre_b, shard * FF_LOC, FF_LOC, axis=1)
            hidden_s = lax.dynamic_slice_in_dim(hidden, shard * FF_LOC, FF_LOC, axis=1)
            context_s = lax.dynamic_slice_in_dim(context, shard * QP, QP, axis=1)
            d_qkv_s = lax.dynamic_slice_in_dim(d_qkv, shard * 3 * QP, 3 * QP, axis=1)
            g_qkv = dot(d_qkv_s, act_in, CONTRACT_ROWS).reshape(3, QP, D)[:, :QW].reshape(3 * QW, D)
            g_out = dot(context_s, d_attn, CONTRACT_ROWS)[:QW]
            return g_qkv, g_out, dot(mlp_in, d_pre_s, CONTRACT_ROWS), dot(hidden_s, d_out, CONTRACT_ROWS)

        kept = weight_grads(own_shard)
        sent = weight_grads(1 - own_shard)
        cross = [(z * DP + 2 * k + z // 2, (z ^ 1) * DP + 2 * k + 1 - z // 2) for z in range(TP) for k in range(DP // 2)]
        total = [jnp.where(is_holder, keep, lax.ppermute(send, ALL, cross)) for keep, send in zip(kept, sent)]
        layer_grads[layer] = lax.psum(tuple(total), 'dp')
    d_embed, vec_grads[0], vec_grads[1] = ln_zero_vjp(d_resid)

    counted = (z_rank < 2).astype(F32)
    bias_stack = jnp.stack([bias_grads[layer] for layer in range(LAYERS)], axis=1) * counted
    bias_slots = lax.dynamic_update_slice(jnp.zeros((TP, LAYERS, 2, D), F32), bias_stack, (2 * core, 0, 0, 0))
    vec_stack = jnp.stack([vec_grads[row] for row in range(final_row + 2)]) * (counted * (core == 0))
    small = lax.psum(jnp.concatenate([vec_stack, bias_slots.reshape(TP * LAYERS * 2, D)], axis=0), ALL)
    g_vec = small[:final_row + 2]
    g_bias = lax.dynamic_index_in_dim(small[final_row + 2:].reshape(TP, LAYERS, 2, D), z_rank, keepdims=False)
    g_bqkv = g_bias[:, 0].reshape(LAYERS, 3, QP)[:, :, :QW].reshape(LAYERS, 3, HEADS_LOC, HEAD).transpose(0, 2, 1, 3).reshape(LAYERS, HEADS_LOC, 3 * HEAD)
    g_bup = g_bias[:, 1]

    d_quart_embed = lax.dynamic_slice_in_dim(d_embed, quarter * QUART, QUART)
    d_rows = lax.all_gather(d_quart_embed, ALL, tiled=True)
    row_ids = token_all - z_rank * VOCAB_LOC
    row_ids = jnp.where((row_ids >= 0) & (row_ids < VOCAB_LOC), row_ids, DP * PIECE)
    g_emb = g_head.at[row_ids].add(d_rows, mode='drop')[:VOCAB_LOC]

    def stacked(slot):
        return [layer_grads[layer][slot] for layer in range(LAYERS)]

    g_qkv = jnp.stack([g.reshape(3, HEADS_LOC, HEAD, D).transpose(3, 1, 0, 2).reshape(D, 3 * QW) for g in stacked(0)])
    grads = [g_emb, g_vec, g_qkv, g_bqkv, jnp.stack(stacked(1)), jnp.stack(stacked(2)), g_bup, jnp.stack(stacked(3))]

    sq_sharded = sum(jnp.sum(grads[slot] * grads[slot]) for slot in range(8) if slot != 1)
    sq_total = lax.psum(sq_sharded, 'tp') + jnp.sum(g_vec * g_vec)
    clip_coef = jnp.minimum(1.0, CLIP_NORM / (jnp.sqrt(sq_total) + 1e-6))
    updated = [adam_update(masters[slot], grads[slot] * clip_coef, moms[slot], vels[slot], DECAYED[slot]) for slot in range(8)]
    new_masters = [entry[0] for entry in updated]
    new_moms = [entry[1] for entry in updated]
    new_vels = [entry[2] for entry in updated]
    new_bf16 = [entry.astype(BF16) for entry in new_masters]
    return (loss, *new_masters, *new_moms, *new_vels, *new_bf16)


def solution(mesh):
    data_spec = P('dp', None)
    return jax.shard_map(device_step, mesh=mesh, in_specs=(data_spec, data_spec) + PARAM_SPECS * 3, out_specs=(P(),) + PARAM_SPECS * 4, check_vma=False)
```

time: 2470 us -> 2440 us (0.988)
  Pallas kernels: 0 us -> 216 us
  matrix products: 291 us -> 104 us
  waiting for transfers between devices: 1680 us -> 1590 us
  local copies, waits for them, and re-layouts: 56 us -> 96.5 us
  other arithmetic: 346 us -> 309 us
    psum x11 -> x4, waiting for transfers between devices: 1680 us -> 574 us  [the longest x1 192 us: device_step(): layer_grads[layer] = lax.psum(tuple(total), 'dp')]
    all_gather x0 -> x5, waiting for transfers between devices: none -> 675 us  [the longest x2 212 us: device_step(): lax.all_gather(pack_weights(w_qkv[l], b_qkv[l], w_out[l], w_up[l], b_up[l...]
    reduce_scatter x0 -> x1, waiting for transfers between devices: none -> 241 us  [device_step(): lax.psum_scatter(d_head_part, ALL, scatter_dimension=0, tiled=True)]
    pallas_call x0 -> x8, Pallas kernels: none -> 216 us  [the longest x1 73.2 us: head_bwd(): pl.pallas_call(head_bwd_kernel, grid=(NTOK // HEAD_TILE,), out_shape=[jax...]
    dot_general x37 -> x32, matrix products: 269 us -> 104 us  [dot(): return lax.dot_general(lhs, rhs, dims, preferred_element_type=F32)]
    ppermute x0 -> x19, waiting for transfers between devices: none -> 97.4 us  [the longest x8 35.7 us: device_step(): lax.ppermute(send, ALL, cross)]
    convert_element_type x18 -> x12, other arithmetic: 194 us -> 129 us  [the longest x8 124 us: device_step(): new_bf16 = [entry.astype(BF16) for entry in new_masters]]
    scatter-add x1, other arithmetic: 34 us -> 78.3 us  [device_step(): g_emb = g_head.at[row_ids].add(d_rows, mode='drop')[:VOCAB_LOC]]
  transfers between devices with their start and end apart: 11 -> 29, of which waited for: 11 -> 20; matrix products, arithmetic and copies ran while one was open for 3% -> 7% of each run, Pallas kernels for 0% -> 2%
where the time goes in v1:
time: 2440 us
  waiting for transfers between devices  1590 us (65%)
  other arithmetic  309 us (13%)
  Pallas kernels  216 us (9%)
  matrix products  104 us (4%)
  local copies, waits for them, and re-layouts  96.5 us (4%)
  blocking collectives  58.9 us (2%)
  starting transfers between devices  37.1 us (2%)
  between operations  26.1 us (1%)
    reduce_scatter x1, waiting for transfers between devices, device_step(): lax.psum_scatter(d_head_part, ALL, scatter_dimension=0, tiled=True)  241 us
    all_gather x2, waiting for transfers between devices, device_step(): lax.all_gather(pack_weights(w_qkv[l], b_qkv[l], w_out[l], w_up[l], b_up[l...  212 us
    psum x1, waiting for transfers between devices, device_step(): layer_grads[layer] = lax.psum(tuple(total), 'dp')  192 us
    all_gather x1, waiting for transfers between devices, device_step(): g_head = lax.all_gather(g_piece[:PIECE], 'dp', tiled=True)  171 us
    all_gather x1, waiting for transfers between devices, device_step(): d_rows = lax.all_gather(d_quart_embed, ALL, tiled=True)  157 us
    psum x1, waiting for transfers between devices, device_step(): x_own = lax.psum(jnp.where(in_shard[:, None], picked, 0.0), 'tp')  143 us
    all_gather x1, waiting for transfers between devices, device_step(): xhat_all = lax.all_gather(xhat, ALL, tiled=True)  135 us
    psum x1, waiting for transfers between devices, device_step(): lax.psum(jnp.stack([stat_loc[1] * jnp.exp(stat_loc[0] - glob_max), stat_l...  128 us
  transfers between devices with their start and end apart: 29, of which 20 were waited for; matrix products, arithmetic and copies ran while one was open for 7% of the time, Pallas kernels for 2%

profile of v1, /device:TPU:0, one launch (start us, length us, event | category | flops | bytes accessed | tf_op | source)
XLA Modules:
  0.0 2435.3 jit_solution(12911046768557287066)
XLA Ops:
  9.5 17.8 gather_fusion
  27.4 3.7 reduce-precision_select_fusion
  34.8 4.2 fusion.135
  40.8 3.5 concatenate.33
  46.8 4.2 concatenate.34
  51.1 143.3 %all-reduce.9.cloned.1.call-done = f32[1024,768]{1,0:T(8,128)} async-done(((f32[1024,768]{1,0:T(8,128)}), f32[1024,768]{1,0:T(8,128)}) %all-reduce.9.cloned.1.call-update) | async-done | bytes 3145744 | tf_op jit(solution)/shard_map/psum | solution.py:389
  209.7 88.0 %all-gather.16.cloned.1.call-done = f32[9472,768]{1,0:T(8,128)} async-done(((f32[296,768]{1,0:T(8,128)}), f32[9472,768]{1,0:T(8,128)}) %all-gather.16.cloned.1.call-update) | async-done | bytes 29098000 | tf_op jit(solution)/shard_map/all_gather | solution.py:391
  297.7 5.6 unpack_weights.2
  306.2 5.4 add_convert_fusion.1.qkv_ref
  311.6 9.7 attn_fwd.2
  324.3 5.3 collective-permute-done.1
  329.7 4.9 fusion.132
  337.7 5.5 multiply_convert_fusion.1
  343.2 4.3 fusion.143
  347.7 124.2 %all-gather.18.cloned.1.call-done = f32[9472,768]{1,0:T(8,128)} async-done(((f32[296,768]{1,0:T(8,128)}), f32[9472,768]{1,0:T(8,128)}) %all-gather.18.cloned.1.call-update) | async-done | bytes 29098000 | tf_op jit(solution)/shard_map/all_gather | solution.py:391
  471.9 5.6 unpack_weights.3
  480.4 5.1 fusion.131
  491.2 9.9 attn_fwd.3
  504.1 5.4 collective-permute-done.3
  509.4 4.3 fusion.130
  516.8 5.3 multiply_convert_fusion
  522.2 4.3 fusion.145
  526.7 5.4 collective-permute-done.4
  532.1 4.3 fusion.129
  542.6 9.2 all-gather.3
  556.0 134.9 %all-gather.10.cloned.1.call-done.xhat_ref = f32[8192,768]{1,0:T(8,128)} async-done(((f32[256,768]{1,0:T(8,128)}), f32[8192,768]{1,0:T(8,128)}) %all-gather.10.cloned.1.call-update) | async-done | bytes 25165840 | tf_op jit(solution)/shard_map/all_gather | solution.py:422
  691.0 67.3 %head_fwd.1 = (bf16[8192,768]{1,0:T(8,128)(2,1)}, f32[1664,8192]{1,0:T(8,128)}, f32[8,8192]{1,0:T(8,128)S(1)}) custom-call(s32[1]{0:T(128)} %bitcast.valid_ref, f32[8192,768]{1,0:T(8,128)} %all-gather.10.cloned.1.call-done.xhat_ref, f32[1,768]{1,0:T(1,128)S(1)} %get-tuple-element.211.gain_ref, f32[1,768]{1,0:T(1,128)S(1)} %get-tuple-element.210.bias_ref, ...), custom_call_target="tpu_custom_call" | custom-call | flops 20937965568 | bytes 100663296 | tf_op jit(solution)/shard_map/head_fwd/pallas_call | solution.py:310
  758.4 38.6 %pmax.7 = f32[8192]{0:T(1024)S(1)} all-reduce(f32[8192]{0:T(1024)S(1)} %bitcast.208), channel_id=1, replica_groups=mesh['tp'=4,'dp'=8] {'tp','dp'}, use_global_device_ids=true, to_apply=%region_13.14 | all-reduce | flops 8192 | bytes 65536 | tf_op jit(solution)/shard_map/pmax | solution.py:438
  797.9 127.7 %all-reduce.11.cloned.1.call-done = f32[2,8192]{1,0:T(2,128)} async-done(((f32[2,8192]{1,0:T(2,128)}), f32[2,8192]{1,0:T(2,128)}) %all-reduce.11.cloned.1.call-update) | async-done | bytes 65552 | tf_op jit(solution)/shard_map/psum | solution.py:439
  927.4 73.2 %head_bwd.1 = (f32[8192,768]{1,0:T(8,128)}, f32[1664,768]{1,0:T(8,128)}) custom-call(f32[1664,8192]{1,0:T(8,128)} %get-tuple-element.63.logit_ref, bf16[8192,768]{1,0:T(8,128)(2,1)} %get-tuple-element.64.head_ref, bf16[1664,768]{1,0:T(8,128)(2,1)S(1)} %pad.13.emb_ref, s32[1,8192]{1,0:T(1,128)S(1)} %compare_select_fusion.1.lab_ref, ...), custom_call_target="tpu_custom_call" | custom-call | flops 41875931136 | bytes 100663296 | tf_op jit(solution)/shard_map/head_bwd/pallas_call | solution.py:338
  1000.7 241.2 %reduce-scatter.2.cloned.1.call-done = f32[256,768]{1,0:T(8,128)} async-done(((f32[8192,768]{1,0:T(8,128)}), f32[256,768]{1,0:T(8,128)}) %reduce-scatter.2.cloned.1.call-update) | async-done | bytes 786448 | tf_op jit(solution)/shard_map/reduce_scatter | solution.py:443
  1243.6 34.1 %collective-permute-done.5 = f32[256,768]{1,0:T(8,128)S(1)} collective-permute-done((f32[256,768]{1,0:T(8,128)}, f32[256,768]{1,0:T(8,128)S(1)}, u32[]{:S(2)}, u32[]{:S(2)}) %collective-permute-start.5) | collective-permute-done | bytes 786464 | tf_op jit(solution)/shard_map/ppermute | solution.py:444
  1293.4 6.8 fusion.121
  1303.1 5.5 collective-permute-done.7
  1315.4 22.4 attn_bwd.2
  1337.9 4.3 fusion.147
  1342.4 4.9 fusion.25
  1356.3 3.8 multiply_reduce_fusion.5
  1364.5 6.5 fusion.134
  1371.0 4.3 fusion.148
  1377.1 4.9 select_bitcast_fusion.2
  1382.0 18.7 collective-permute-done.18
  1405.2 7.0 collective-permute-start.12
  1426.3 3.7 multiply_reduce_fusion.6
  1435.6 22.0 attn_bwd.3
  1457.6 4.3 fusion.149
  1470.1 4.4 select_bitcast_fusion.3
  1474.5 13.3 collective-permute-done.17
  1491.4 6.6 collective-permute-start.13
  1506.4 3.4 fusion.50
  1509.9 4.1 multiply_reduce_fusion.7
  1519.8 3.7 collective-permute-done.11
  1525.3 4.9 slice.219
  1536.8 111.1 %all-reduce.13.cloned.1.call-done = f32[32,768]{1,0:T(8,128)} async-done(((f32[32,768]{1,0:T(8,128)}), f32[32,768]{1,0:T(8,128)}) %all-reduce.13.cloned.1.call-update) | async-done | bytes 98320 | tf_op jit(solution)/shard_map/psum | solution.py:496
  1651.3 191.9 %all-reduce.15.cloned.1.call-done = (f32[1,768,576]{1,2,0:T(8,128)}, f32[1,768,576]{1,2,0:T(8,128)}, f32[1,192,768]{2,1,0:T(8,128)}, f32[1,192,768]{2,1,0:T(8,12...) async-done(((f32[1,768,576]{1,2,0:T(8,128)}, f32[1,768,576]{1,2,0:T(8,128)}, f32[1,192,768]{2,1,0:T(8,128)}, ...) | async-done | bytes 14155792 | tf_op jit(solution)/shard_map/psum | solution.py:489
  1858.1 171.1 %all-gather.12.cloned.1.call-done = f32[12608,768]{1,0:T(8,128)} async-done(((f32[1576,768]{1,0:T(8,128)}), f32[12608,768]{1,0:T(8,128)}) %all-gather.12.cloned.1.call-update) | async-done | bytes 38731792 | tf_op jit(solution)/shard_map/all_gather | solution.py:448
  2029.3 156.6 %all-gather.14.cloned.1.call-done = f32[8192,768]{1,0:T(8,128)} async-done(((f32[256,768]{1,0:T(8,128)}), f32[8192,768]{1,0:T(8,128)}) %all-gather.14.cloned.1.call-update) | async-done | bytes 25165840 | tf_op jit(solution)/shard_map/all_gather | solution.py:503
  2185.9 78.3 %scatter_fusion = f32[12608,768]{1,0:T(8,128)} fusion(f32[12608,768]{1,0:T(8,128)} %all-gather.12.cloned.1.call-done, s32[8192]{0:T(1024)S(1)} %bitcast.216, f32[8192,768]{1,0:T(8,128)} %all-gather.14.cloned.1.call-done), kind=kCustom, calls=%fused_computation.1 | custom fusion | flops 6291456 | bytes 75530240 | tf_op jit(solution)/shard_map/scatter-add | solution.py:506
  2264.3 17.6 multiply_reduce_fusion
  2287.1 11.1 psum.95
  2299.7 90.5 %fusion.115 = (bf16[12576,768]{1,0:T(8,128)(2,1)}, f32[12576,768]{1,0:T(8,128)}, f32[12576,768]{1,0:T(8,128)}, f32[12576,768]{1,0:T(8,128)}) fusion(f32[12576,768]{1,0:T(8,128)} %param.29, f32[]{:T(128)S(6)} %min.30, f32[12608,768]{1,0:T(8,128)} %scatter_fusion, f32[12576,768]{1,0:T(8,128)} %param.37, f32[12576,768]{1,0:T(8,128)} %param.45), kind=kLoop, calls=%fused_computation.295 | loop fusion | flops 164192256 | bytes 289751040 | tf_op jit(solution)/shard_map/convert_element_type | solution.py:521
  2390.3 9.3 fusion.111
  2404.3 10.4 fusion.105
  2415.5 9.5 fusion.100
  (591 shorter events, 186.8 us)
Async XLA Ops:
  8.0 186.3 %all-reduce.9.cloned.1.call-start = ((), (), s32[]{:S(2)}) async-start(), calls=%async_computation.1 | async-start | bytes 6291456 | tf_op jit(solution)/shard_map/psum | solution.py:389
  31.0 266.7 %all-gather.16.cloned.1.call-start = ((), (), s32[]{:S(2)}) async-start(), calls=%async_computation.8 | async-start | bytes 30007296 | tf_op jit(solution)/shard_map/all_gather | solution.py:391
  44.3 427.5 %all-gather.18.cloned.1.call-start = ((), (), s32[]{:S(2)}) async-start(), calls=%async_computation.9 | async-start | bytes 30007296 | tf_op jit(solution)/shard_map/all_gather | solution.py:391
  44.5 152.8 %copy-start.153 = (f32[12]{0:T(128)S(1)}, f32[12]{0:T(128)}, u32[]{:S(2)}) copy-start(f32[12]{0:T(128)} %constant.244.clone) | copy-start | bytes 148
  44.5 152.8 %copy-start.96 = (f32[16,768]{1,0:T(8,128)S(1)}, f32[16,768]{1,0:T(8,128)}, u32[]{:S(2)}) copy-start(f32[16,768]{1,0:T(8,128)} %param.30) | copy-start | bytes 147460
  51.0 640.0 %all-gather.10.cloned.1.call-start = ((), (), s32[]{:S(2)}) async-start(), calls=%async_computation.2 | async-start | bytes 25952256 | tf_op jit(solution)/shard_map/all_gather | solution.py:422
  194.3 6.6 collective-permute-start
  198.0 131.6 %copy-start.88 = (f32[768]{0:T(1024)}, f32[768]{0:T(1024)S(1)}, u32[]{:S(2)}) copy-start(f32[768]{0:T(1024)S(1)} %get-tuple-element.104) | copy-start | bytes 9220
  198.0 131.6 %copy-start.94 = (f32[768]{0:T(1024)}, f32[768]{0:T(1024)S(1)}, u32[]{:S(2)}) copy-start(f32[768]{0:T(1024)S(1)} %get-tuple-element.103) | copy-start | bytes 9220
  198.0 137.1 %copy-start.111 = (f32[768]{0:T(1024)}, f32[768]{0:T(1024)S(1)}, u32[]{:S(2)}) copy-start(f32[768]{0:T(1024)S(1)} %get-tuple-element.99) | copy-start | bytes 9220
  198.0 288.0 %copy-start.113 = (f32[768]{0:T(1024)}, f32[768]{0:T(1024)S(1)}, u32[]{:S(2)}) copy-start(f32[768]{0:T(1024)S(1)} %get-tuple-element.96) | copy-start | bytes 9220
  203.2 126.5 %copy-start.86 = (f32[1024]{0:T(1024)}, f32[1024]{0:T(1024)S(1)}, u32[]{:S(2)}) copy-start(f32[1024]{0:T(1024)S(1)} %broadcast_multiply_fusion.6) | copy-start | bytes 12292
  203.7 125.9 %copy-start.90 = (f32[1024]{0:T(1024)}, f32[1024]{0:T(1024)S(1)}, u32[]{:S(2)}) copy-start(f32[1024]{0:T(1024)S(1)} %fusion.81) | copy-start | bytes 12292
  206.4 97.0 %copy-start.125 = (f32[1024]{0:T(1024)}, f32[1024]{0:T(1024)S(1)}, u32[]{:S(2)}) copy-start(f32[1024]{0:T(1024)S(1)} %multiply_reduce_fusion.19) | copy-start | bytes 12292
  206.4 96.9 %copy-start.115 = (f32[1024]{0:T(1024)}, f32[1024]{0:T(1024)S(1)}, u32[]{:S(2)}) copy-start(f32[1024]{0:T(1024)S(1)} %fusion.82) | copy-start | bytes 12292
  306.2 15.2 copy-start.4
  324.0 5.6 collective-permute-start.1
  324.3 11.9 copy-start.146
  347.5 132.9 %collective-permute-start.2 = (f32[1024,768]{1,0:T(8,128)}, f32[1024,768]{1,0:T(8,128)}, u32[]{:S(2)}, u32[]{:S(2)}) collective-permute-start(f32[1024,768]{1,0:T(8,128)} %fusion.143), channel_id=1, source_target_pairs={{0,1},{1,0},{2,3},{3,2},{4,5},{5,4},{6,7},{7,6},{8,9},{9,8},{10,11... | collective-permute-start | bytes 9437192 | tf_op jit(solution)/shard_map/ppermute | solution.py:357
  503.8 5.6 collective-permute-start.3
  526.5 5.6 collective-permute-start.4
  539.0 386.7 %all-reduce.11.cloned.1.call-start = ((), (), s32[]{:S(2)}) async-start(), calls=%async_computation.3 | async-start | bytes 131072 | tf_op jit(solution)/shard_map/psum | solution.py:439
  797.0 203.6 %copy-start.84 = (f32[8192]{0:T(1024)}, f32[8192]{0:T(1024)S(1)}, u32[]{:S(2)}) copy-start(f32[8192]{0:T(1024)S(1)} %pmax.7) | copy-start | bytes 98308
  797.8 444.1 %reduce-scatter.2.cloned.1.call-start = ((), (), s32[]{:S(2)}) async-start(), calls=%async_computation.5 | async-start | bytes 25952256 | tf_op jit(solution)/shard_map/reduce_scatter | solution.py:443
  1000.6 647.3 %all-reduce.13.cloned.1.call-start = ((), (), s32[]{:S(2)}) async-start(), calls=%async_computation.7 | async-start | bytes 196608 | tf_op jit(solution)/shard_map/psum | solution.py:496
  1241.9 38.6 %copy-start.68 = (f32[256,768]{1,0:T(8,128)S(1)}, f32[256,768]{1,0:T(8,128)}, u32[]{:S(2)}) copy-start(f32[256,768]{1,0:T(8,128)} %reduce-scatter.2.cloned.1.call-done) | copy-start | bytes 2359300
  1241.9 35.9 %collective-permute-start.5 = (f32[256,768]{1,0:T(8,128)}, f32[256,768]{1,0:T(8,128)S(1)}, u32[]{:S(2)}, u32[]{:S(2)}) collective-permute-start(f32[256,768]{1,0:T(8,128)} %reduce-scatter.2.cloned.1.call-done), channel_id=1, source_target_pairs={{0,16},{1,17},{2,18},{3,19},{4,20},{5,21},{6,22},{7,23},{8,24},{9,... | collective-permute-start | bytes 2359304 | tf_op jit(solution)/shard_map/ppermute | solution.py:444
  1280.4 3.4 collective-permute-start.6
  1302.8 5.7 collective-permute-start.7
  1315.4 22.5 copy-start.15
  1337.9 65.7 %copy-start.22 = (bf16[1024,1536]{1,0:T(8,128)(2,1)}, bf16[1024,1536]{1,0:T(8,128)(2,1)S(1)}, u32[]{:S(2)}) copy-start(bf16[1024,1536]{1,0:T(8,128)(2,1)S(1)} %get-tuple-element.67) | copy-start | bytes 9437188
  1342.2 14.1 collective-permute-start.8
  1347.3 29.9 %collective-permute-start.16 = (f32[768,768]{1,0:T(8,128)}, f32[768,768]{1,0:T(8,128)}, u32[]{:S(2)}, u32[]{:S(2)}) collective-permute-start(f32[768,768]{1,0:T(8,128)} %fusion.25), channel_id=1, source_target_pairs={{0,9},{2,11},{4,13},{6,15},{8,1},{10,3},{12,5},{14,7},{17,24},{19,... | collective-permute-start | bytes 7077896 | tf_op jit(solution)/shard_map/ppermute | solution.py:488
  1353.4 47.3 %collective-permute-start.18 = (f32[768,768]{1,0:T(8,128)}, f32[768,768]{1,0:T(8,128)}, u32[]{:S(2)}, u32[]{:S(2)}) collective-permute-start(f32[768,768]{1,0:T(8,128)} %fusion.17), channel_id=1, source_target_pairs={{0,9},{2,11},{4,13},{6,15},{8,1},{10,3},{12,5},{14,7},{17,24},{19,... | collective-permute-start | bytes 7077896 | tf_op jit(solution)/shard_map/ppermute | solution.py:488
  1375.3 51.0 %collective-permute-start.9 = (f32[1024,768]{1,0:T(8,128)}, f32[1024,768]{1,0:T(8,128)}, u32[]{:S(2)}, u32[]{:S(2)}) collective-permute-start(f32[1024,768]{1,0:T(8,128)} %fusion.148), channel_id=1, source_target_pairs={{0,1},{1,0},{2,3},{3,2},{4,5},{5,4},{6,7},{7,6},{8,9},{9,8},{10,11... | collective-permute-start | bytes 9437192 | tf_op jit(solution)/shard_map/ppermute | solution.py:357
  1377.1 23.6 copy-start.81
  1377.1 23.6 copy-start.159
  1382.0 21.6 copy-start.77
  1405.2 61.6 %collective-permute-start.12 = (f32[576,768]{1,0:T(8,128)S(1)}, f32[576,768]{1,0:T(8,128)}, u32[]{:S(2)}, u32[]{:S(2)}) collective-permute-start(f32[576,768]{1,0:T(8,128)S(1)} %bitcast.200), channel_id=1, source_target_pairs={{0,9},{2,11},{4,13},{6,15},{8,1},{10,3},{12,5},{14,7},{17,24},{19,... | collective-permute-start | bytes 5308424 | tf_op jit(solution)/shard_map/ppermute | solution.py:488
  1412.8 52.4 %collective-permute-start.14 = (f32[192,768]{1,0:T(8,128)S(1)}, f32[192,768]{1,0:T(8,128)S(1)}, u32[]{:S(2)}, u32[]{:S(2)}) collective-permute-start(f32[192,768]{1,0:T(8,128)S(1)} %fusion.52), channel_id=1, source_target_pairs={{0,9},{2,11},{4,13},{6,15},{8,1},{10,3},{12,5},{14,7},{17,24},{19,... | collective-permute-start | bytes 1769480 | tf_op jit(solution)/shard_map/ppermute | solution.py:488
  1417.5 52.6 %collective-permute-start.15 = (f32[768,768]{1,0:T(8,128)}, f32[768,768]{1,0:T(8,128)}, u32[]{:S(2)}, u32[]{:S(2)}) collective-permute-start(f32[768,768]{1,0:T(8,128)} %fusion.29), channel_id=1, source_target_pairs={{0,9},{2,11},{4,13},{6,15},{8,1},{10,3},{12,5},{14,7},{17,24},{19,... | collective-permute-start | bytes 7077896 | tf_op jit(solution)/shard_map/ppermute | solution.py:488
  1423.4 64.4 %collective-permute-start.17 = (f32[768,768]{1,0:T(8,128)}, f32[768,768]{1,0:T(8,128)}, u32[]{:S(2)}, u32[]{:S(2)}) collective-permute-start(f32[768,768]{1,0:T(8,128)} %fusion.21), channel_id=1, source_target_pairs={{0,9},{2,11},{4,13},{6,15},{8,1},{10,3},{12,5},{14,7},{17,24},{19,... | collective-permute-start | bytes 7077896 | tf_op jit(solution)/shard_map/ppermute | solution.py:488
  1432.5 25.0 %copy-start.44 = (f32[1024,768]{1,0:T(8,128)}, f32[1024,768]{1,0:T(8,128)S(1)}, u32[]{:S(2)}) copy-start(f32[1024,768]{1,0:T(8,128)S(1)} %get-tuple-element.158) | copy-start | bytes 9437188
  1435.6 22.0 copy-start.7
  1461.9 47.9 %collective-permute-start.10 = (f32[1024,768]{1,0:T(8,128)}, f32[1024,768]{1,0:T(8,128)}, u32[]{:S(2)}, u32[]{:S(2)}) collective-permute-start(f32[1024,768]{1,0:T(8,128)} %fusion.149), channel_id=1, source_target_pairs={{0,1},{1,0},{2,3},{3,2},{4,5},{5,4},{6,7},{7,6},{8,9},{9,8},{10,11... | collective-permute-start | bytes 9437192 | tf_op jit(solution)/shard_map/ppermute | solution.py:357
  1470.1 17.7 copy-start.59
  1470.1 17.7 copy-start.156
  1474.5 16.2 copy-start.1
  1474.5 16.2 copy-start.45
  1491.4 15.0 collective-permute-start.13
  1500.8 22.7 collective-permute-start.11
  1519.8 323.4 %all-reduce.15.cloned.1.call-start = ((), (), s32[]{:S(2)}) async-start(), calls=%async_computation.10 | async-start | bytes 28311552 | tf_op jit(solution)/shard_map/psum | solution.py:489
  1525.2 504.1 %all-gather.12.cloned.1.call-start = ((), (), s32[]{:S(2)}) async-start(), calls=%async_computation.4 | async-start | bytes 43573248 | tf_op jit(solution)/shard_map/all_gather | solution.py:448
  1530.2 655.7 %all-gather.14.cloned.1.call-start = ((), (), s32[]{:S(2)}) async-start(), calls=%async_computation.6 | async-start | bytes 25952256 | tf_op jit(solution)/shard_map/all_gather | solution.py:503
  2299.7 90.5 %copy-start.51 = (f32[2,768,576]{1,2,0:T(8,128)S(1)}, f32[2,768,576]{1,2,0:T(8,128)}, u32[]{:S(2)}) copy-start(f32[2,768,576]{1,2,0:T(8,128)} %copy-done.50) | copy-start | bytes 10616836
  2390.3 12.0 copy-start.49
  2390.3 13.9 copy-start.52
  2399.7 15.7 slice-start
  2399.7 15.6 slice-start.4
  2404.2 10.4 copy-start.136
  2404.2 10.4 copy-start.148
  2404.2 10.5 copy-start.149
  2404.2 11.1 slice-start.1
  2404.3 11.1 slice-start.5
  (135 other events, 660.5 us)
Sparse Core Ops, SparseCore 0:
  31.2 163.1 all-reduce.8
Sparse Core Ops, SparseCore 1:
  44.4 253.2 all-gather.15
  301.1 170.7 all-gather.17
  539.0 151.9 all-gather.9
  797.9 127.7 all-reduce.10
  1000.7 241.1 reduce-scatter.1
  1519.9 128.0 all-reduce.12
  1655.4 187.7 all-reduce.14
  1845.5 183.7 all-gather.11
  2032.6 153.2 all-gather.13
